TPU v7x, 32 devices: a whole 2x2x4 slice. The times are simulated.
32 devices in a mesh: dp: 8 (over y, x, core), tensor: 4 (over z).
Axes of the slice: x: 2, y: 2, z: 4, core: 2. Of those that a mesh axis runs over, the one named last changes fastest.
Arguments:
- tokens: bfloat16 [8192, 1536], P(('dp', 'tensor')), may hold values from -6 to 6
- segment_ids: int32 [8, 1024], P('dp'), may hold values from 0 to 3, never falling along the last dimension, each value on 1 to 512 neighbouring positions
- cotangent: bfloat16 [8192, 1536], P(('dp', 'tensor')), may hold values from -6 to 6
- norm_gain: bfloat16 [1536], P(('dp', 'tensor')), may hold values from 0.5 to 1.5
- w_zx: bfloat16 [1536, 2, 3072], P('dp', None, 'tensor'), may hold values from -0.15625 to 0.15625
- w_bc: bfloat16 [1536, 256], P(('dp', 'tensor')), may hold values from -0.15625 to 0.15625
- w_dt: bfloat16 [1536, 48], P('dp', 'tensor'), may hold values from -0.15625 to 0.15625
- conv_x_w: float32 [4, 3072], P(None, 'tensor'), may hold values from -3 to 3
- conv_x_b: float32 [3072], P('tensor'), may hold values from -3 to 3
- conv_bc_w: float32 [4, 256], replicated, may hold values from -3 to 3
- conv_bc_b: float32 [256], replicated, may hold values from -3 to 3
- dt_bias: float32 [48], P('tensor'), may hold values from -6 to -1
- a_log: float32 [48], P('tensor'), may hold values from -4 to 1
- d_skip: float32 [48], P('tensor'), may hold values from 0.5 to 2
- gate_gain: float32 [3072], P('tensor'), may hold values from 0.5 to 1.5
- w_out: bfloat16 [3072, 1536], P('tensor', 'dp'), may hold values from -0.109375 to 0.109375
Outputs:
- layer_out: bfloat16 [8192, 1536], P(('dp', 'tensor'))
- grad_tokens: float32 [8192, 1536], P(('dp', 'tensor'))
- grad_norm_gain: float32 [1536], P(('dp', 'tensor'))
- grad_w_zx: float32 [1536, 2, 3072], P('dp', None, 'tensor')
- grad_w_bc: float32 [1536, 256], P(('dp', 'tensor'))
- grad_w_dt: float32 [1536, 48], P('dp', 'tensor')
- grad_conv_x_w: float32 [4, 3072], P(None, 'tensor')
- grad_conv_x_b: float32 [3072], P('tensor')
- grad_conv_bc_w: float32 [4, 256], replicated
- grad_conv_bc_b: float32 [256], replicated
- grad_dt_bias: float32 [48], P('tensor')
- grad_a_log: float32 [48], P('tensor')
- grad_d_skip: float32 [48], P('tensor')
- grad_gate_gain: float32 [3072], P('tensor')
- grad_w_out: float32 [3072, 1536], P('tensor', 'dp')
Inputs may be any that keep to these rules, and one draw needn't show every extreme that they name: `segment_ids`: document numbers start at 0 in each sequence and never fall along it; every document holds 1 to half of 1024 positions, and some document holds exactly that many.
All inputs are finite; a program needn't handle non-finite values.
Results may differ from a plain program's by a relative error of at most 0.012.
Values may be sent and summed in bfloat16 or wider, within the bound.
A program may use at most 192 MiB of HBM per device.

v0:
```python
import jax
import jax.numpy as jnp
from jax import lax
from jax.sharding import PartitionSpec as P

HEADS = 48
HEAD_DIM = 64
STATE = 128
BLOCK = 256


EPSILON = 1e-05
HIGHEST = lax.Precision.HIGHEST


def silu_grad(values):
    sigmoid_v = jax.nn.sigmoid(values)
    return sigmoid_v * (1.0 + values * (1.0 - sigmoid_v))


def causal_conv(values, kernel, offset, segment):
    length = values.shape[0]
    width = kernel.shape[0]
    padded = jnp.concatenate([jnp.zeros((width - 1, values.shape[1]), jnp.float32), values], 0)
    seg_pad = jnp.concatenate([jnp.full((width - 1,), -1, jnp.int32), segment], 0)
    summed = jnp.zeros(values.shape, jnp.float32) + offset
    for shift_by in range(width):
        shifted = padded[width - 1 - shift_by : width - 1 - shift_by + length]
        same_doc = (
            seg_pad[width - 1 - shift_by : width - 1 - shift_by + length] == segment
        ).astype(jnp.float32)
        summed = summed + kernel[shift_by] * shifted * same_doc[:, None]
    return summed


def mixer_sequence(conv_in, bc_act, dt_pre, conv_x_w, conv_x_b, dt_bias, a_log, d_skip, segment):
    length = conv_in.shape[0]
    head_count = dt_pre.shape[1]
    blocks = length // BLOCK
    conv_act = jax.nn.silu(causal_conv(conv_in, conv_x_w, conv_x_b, segment)).reshape(
        blocks, BLOCK, head_count, HEAD_DIM
    )
    input_mat = bc_act[:, :STATE].reshape(blocks, BLOCK, STATE)
    output_mat = bc_act[:, STATE:].reshape(blocks, BLOCK, STATE)
    step_size = jax.nn.softplus(dt_pre + dt_bias).reshape(blocks, BLOCK, head_count)
    log_decay = step_size * -jnp.exp(a_log)
    cumulative = jnp.cumsum(log_decay, axis=1)
    cum_heads = jnp.transpose(cumulative, (0, 2, 1))
    seg_blocks = segment.reshape(blocks, BLOCK)
    places = jnp.arange(BLOCK)
    visible = (places[None, :] <= places[:, None])[None] & (
        seg_blocks[:, None, :] == seg_blocks[:, :, None]
    )
    exponent = cum_heads[:, :, :, None] - cum_heads[:, :, None, :]
    decay = jnp.exp(jnp.where(visible[:, None], exponent, 0.0)) * visible[:, None].astype(
        jnp.float32
    )
    scores = jnp.einsum("btn,bsn->bts", output_mat, input_mat, precision=HIGHEST)
    weighted = conv_act * step_size[..., None]
    within = jnp.einsum("bhts,bshp->bthp", decay * scores[:, None], weighted, precision=HIGHEST)
    last_seg = seg_blocks[:, -1]
    keep_end = (seg_blocks == last_seg[:, None]).astype(jnp.float32)
    to_end = jnp.exp(cumulative[:, -1:, :] - cumulative) * keep_end[..., None]
    states = jnp.einsum(
        "bsn,bshp->bhnp", input_mat, weighted * to_end[..., None], precision=HIGHEST
    )
    prev_seg = jnp.concatenate([jnp.full((1,), -1, jnp.int32), last_seg[:-1]], 0)
    block_decay = jnp.exp(cumulative[:, -1, :])
    carry_keep = (last_seg == prev_seg).astype(jnp.float32)

    def carry_step(carried, items):
        own_state, decay_here, keep_here = items
        updated = own_state + (decay_here * keep_here)[:, None, None] * carried
        return (updated, carried)

    _, incoming = lax.scan(
        carry_step,
        jnp.zeros((head_count, STATE, HEAD_DIM), jnp.float32),
        (states, block_decay, carry_keep),
    )
    from_prev = (seg_blocks == prev_seg[:, None]).astype(jnp.float32)[..., None] * jnp.exp(
        cumulative
    )
    from_before = (
        jnp.einsum("btn,bhnp->bthp", output_mat, incoming, precision=HIGHEST) * from_prev[..., None]
    )
    result = within + from_before + d_skip[:, None] * conv_act
    return result.reshape(length, head_count * HEAD_DIM)


def body(
    tokens,
    segment_ids,
    cotangent,
    norm_gain,
    w_zx,
    w_bc,
    w_dt,
    conv_x_w,
    conv_x_b,
    conv_bc_w,
    conv_bc_b,
    dt_bias,
    a_log,
    d_skip,
    gate_gain,
    w_out,
):
    inner = HEADS * HEAD_DIM
    own_rows = tokens.shape[0]
    seq_count, length = segment_ids.shape
    gain_full, bc_weight = (
        lax.all_gather(norm_gain, ("dp", "tensor"), axis=0, tiled=True),
        lax.all_gather(w_bc, ("dp", "tensor"), axis=0, tiled=True),
    )
    zx_weight, dt_weight, out_weight = (
        lax.all_gather(w_zx, "dp", axis=0, tiled=True),
        lax.all_gather(w_dt, "dp", axis=0, tiled=True),
        lax.all_gather(w_out, "dp", axis=1, tiled=True),
    )
    model_width = zx_weight.shape[0]
    local_width = zx_weight.shape[2]
    tokens_f = tokens.astype(jnp.float32)
    gain_f = gain_full.astype(jnp.float32)
    inv_rms = lax.rsqrt(jnp.mean(tokens_f * tokens_f, -1, keepdims=True) + EPSILON)
    normed_own = (tokens_f * inv_rms * gain_f).astype(jnp.bfloat16)
    normed_in = lax.all_gather(normed_own, "tensor", axis=0, tiled=True)
    zx_all = jnp.dot(
        normed_in,
        zx_weight.reshape(model_width, 2 * local_width),
        preferred_element_type=jnp.float32,
    )
    gate_pre = zx_all[:, :local_width]
    conv_in = zx_all[:, local_width:]
    bc_pre = jnp.dot(normed_in, bc_weight, preferred_element_type=jnp.float32)
    dt_pre = jnp.dot(normed_in, dt_weight, preferred_element_type=jnp.float32)

    def bc_piece(bc_values, kernel, offset):

        def bc_single(values, segment):
            return jax.nn.silu(causal_conv(values, kernel, offset, segment))

        stacked = jax.vmap(bc_single)(bc_values.reshape(seq_count, length, -1), segment_ids)
        return stacked.reshape(seq_count * length, -1)

    def core_piece(conv_vals, bc_vals, dt_vals, kernel, offset, bias_dt, log_rate, skip):

        def core_single(conv_seq, bc_seq, dt_seq, segment):
            return mixer_sequence(
                conv_seq, bc_seq, dt_seq, kernel, offset, bias_dt, log_rate, skip, segment
            )

        stacked = jax.vmap(core_single)(
            conv_vals.reshape(seq_count, length, -1),
            bc_vals.reshape(seq_count, length, -1),
            dt_vals.reshape(seq_count, length, -1),
            segment_ids,
        )
        return stacked.reshape(seq_count * length, -1)

    bc_act, bc_pull = jax.vjp(bc_piece, bc_pre, conv_bc_w, conv_bc_b)
    core, core_pull = jax.vjp(
        core_piece, conv_in, bc_act, dt_pre, conv_x_w, conv_x_b, dt_bias, a_log, d_skip
    )
    gate_act = jax.nn.silu(gate_pre)
    gated = core * gate_act
    square_sum = lax.psum(jnp.sum(gated * gated, -1), "tensor")
    gate_rms = lax.rsqrt(square_sum / inner + EPSILON)[:, None]
    normed_out = (gated * gate_rms * gate_gain).astype(jnp.bfloat16)
    mixed = jnp.dot(normed_out, out_weight, preferred_element_type=jnp.float32)
    mixed_own = lax.psum_scatter(
        mixed.astype(jnp.bfloat16), "tensor", scatter_dimension=0, tiled=True
    ).astype(jnp.float32)
    layer_out = (tokens_f + mixed_own).astype(jnp.bfloat16)
    zx_back, dt_back, out_back = (
        lax.all_gather(w_zx, "dp", axis=0, tiled=True),
        lax.all_gather(w_dt, "dp", axis=0, tiled=True),
        lax.all_gather(w_out, "dp", axis=1, tiled=True),
    )
    d_out = lax.all_gather(cotangent, "tensor", axis=0, tiled=True)
    d_normed = jnp.einsum("td,cd->tc", d_out, out_back, preferred_element_type=jnp.float32)
    g_out = jnp.einsum("tc,td->cd", normed_out, d_out, preferred_element_type=jnp.float32)
    inner_dot = lax.psum(jnp.sum(gated * gate_gain * d_normed, -1), "tensor")[:, None]
    d_gated = (
        gate_rms * gate_gain * d_normed
        - gated * (gate_rms * gate_rms * gate_rms) * inner_dot / inner
    )
    g_gate_gain = jnp.sum(d_normed * gated * gate_rms, 0)
    d_core = d_gated * gate_act
    d_gate = d_gated * core * silu_grad(gate_pre)
    d_conv_in, d_bc_part, d_dt_pre, g_cxw, g_cxb, g_dtb, g_alog, g_skip = core_pull(d_core)
    d_bc_act = lax.psum(d_bc_part, "tensor")
    d_bc_pre, g_cbw, g_cbb = bc_pull(d_bc_act)
    dz_b = jnp.stack([d_gate, d_conv_in], 1).astype(jnp.bfloat16)
    dt_b = d_dt_pre.astype(jnp.bfloat16)
    input_part = jnp.einsum(
        "tkc,dkc->td", dz_b, zx_back, preferred_element_type=jnp.float32
    ) + jnp.einsum("th,dh->td", dt_b, dt_back, preferred_element_type=jnp.float32)
    d_normed_own = lax.psum_scatter(
        input_part.astype(jnp.bfloat16), "tensor", scatter_dimension=0, tiled=True
    ).astype(jnp.float32)
    row_start = lax.axis_index("tensor") * own_rows
    bc_own = lax.dynamic_slice_in_dim(d_bc_pre, row_start, own_rows, 0).astype(jnp.bfloat16)
    d_normed_own = d_normed_own + jnp.einsum(
        "tn,dn->td", bc_own, bc_weight, preferred_element_type=jnp.float32
    )
    g_zx = jnp.einsum("td,tkc->dkc", normed_in, dz_b, preferred_element_type=jnp.float32)
    g_dt = jnp.einsum("td,th->dh", normed_in, dt_b, preferred_element_type=jnp.float32)
    g_bc = jnp.einsum("td,tn->dn", normed_own, bc_own, preferred_element_type=jnp.float32)
    g_norm = jnp.sum(d_normed_own * tokens_f * inv_rms, 0)
    d_tokens = inv_rms * (gain_f * d_normed_own) - tokens_f * (
        inv_rms * inv_rms * inv_rms
    ) * jnp.mean(tokens_f * gain_f * d_normed_own, -1, keepdims=True)
    grad_tokens = cotangent.astype(jnp.float32) + d_tokens
    grad_zx, grad_dt, grad_out = (
        lax.psum_scatter(g_zx.astype(jnp.bfloat16), "dp", scatter_dimension=0, tiled=True).astype(
            jnp.float32
        ),
        lax.psum_scatter(g_dt.astype(jnp.bfloat16), "dp", scatter_dimension=0, tiled=True).astype(
            jnp.float32
        ),
        lax.psum_scatter(g_out.astype(jnp.bfloat16), "dp", scatter_dimension=1, tiled=True).astype(
            jnp.float32
        ),
    )
    grad_bc, grad_norm = (
        lax.psum_scatter(g_bc, ("dp", "tensor"), scatter_dimension=0, tiled=True),
        lax.psum_scatter(g_norm, ("dp", "tensor"), scatter_dimension=0, tiled=True),
    )
    summed = lax.psum((g_cxw, g_cxb, g_dtb, g_alog, g_skip, g_gate_gain, g_cbw, g_cbb), "dp")
    grad_cxw, grad_cxb, grad_dtb, grad_alog, grad_skip, grad_gate, grad_cbw, grad_cbb = summed
    return (
        layer_out,
        grad_tokens,
        grad_norm,
        grad_zx,
        grad_bc,
        grad_dt,
        grad_cxw,
        grad_cxb,
        grad_cbw,
        grad_cbb,
        grad_dtb,
        grad_alog,
        grad_skip,
        grad_gate,
        grad_out,
    )


def solution(mesh):
    in_specs = (
        P(("dp", "tensor"), None),
        P("dp", None),
        P(("dp", "tensor"), None),
        P(("dp", "tensor")),
        P("dp", None, "tensor"),
        P(("dp", "tensor"), None),
        P("dp", "tensor"),
        P(None, "tensor"),
        P("tensor"),
        P(),
        P(),
        P("tensor"),
        P("tensor"),
        P("tensor"),
        P("tensor"),
        P("tensor", "dp"),
    )
    out_specs = (
        P(("dp", "tensor"), None),
        P(("dp", "tensor"), None),
        P(("dp", "tensor")),
        P("dp", None, "tensor"),
        P(("dp", "tensor"), None),
        P("dp", "tensor"),
        P(None, "tensor"),
        P("tensor"),
        P(),
        P(),
        P("tensor"),
        P("tensor"),
        P("tensor"),
        P("tensor"),
        P("tensor", "dp"),
    )
    return jax.shard_map(body, mesh=mesh, in_specs=in_specs, out_specs=out_specs, check_vma=False)
```

profile of v0, /device:TPU:0, one launch (start us, length us, event | category | flops | bytes accessed | tf_op | source)
XLA Modules:
  0.0 849.2 jit_solution(17170480090893746734)
XLA Ops:
  10.2 42.0 %all-reduce.23 = bf16[1536]{0:T(1024)(128)(2,1)S(1)} all-reduce(bf16[1536]{0:T(1024)(128)(2,1)S(1)} %dynamic-update-slice), channel_id=1, replica_groups=mesh['dp'=8,'tensor'=4] {'dp','tensor'}, use_global_device_ids=true, to_apply=%add.23 | all-reduce | flops 1536 | bytes 6144
  52.8 2.3 fusion.57
  59.2 10.0 %all-gather = bf16[8,192,12]{1,2,0:T(8,128)(2,1)S(1)} all-gather(bf16[1,192,12]{1,2,0:T(8,128)(2,1)S(1)} %bitcast.381), channel_id=1, replica_groups=mesh['dp'=8,'tensor'=4] {'dp'}, dimensions={0}, use_global_device_ids=true | all-gather | bytes 41472 | tf_op jit(solution)/shard_map/all_gather | solution.py:118
  69.4 83.5 %all_gather.28 = bf16[1536,256]{1,0:T(8,128)(2,1)S(1)} all-gather(bf16[48,256]{1,0:T(8,128)(2,1)S(1)} %copy-done.52), channel_id=1, replica_groups=mesh['dp'=8,'tensor'=4] {'dp','tensor'}, dimensions={0}, use_global_device_ids=true | all-gather | bytes 811008 | tf_op jit(solution)/shard_map/all_gather | solution.py:114
  154.5 3.4 compare_select_fusion.2
  158.2 2.5 reduce-window.14
  162.7 2.9 fusion.145
  167.7 2.0 fusion.146
  170.4 6.6 copy.394
  177.0 8.0 fusion.144
  185.4 2.4 copy-done.2
  187.7 4.3 fusion.40
  192.1 3.6 copy.395
  195.7 5.1 reshape.855
  200.8 5.2 reshape.869
  206.0 6.2 fusion.77
  212.2 2.0 broadcast.354.clone
  214.2 23.0 %while.36 = (s32[]{:T(128)}, f32[1,12,128,64]{3,2,1,0:T(8,128)S(1)}, f32[4,1,12,128,64]{4,3,2,1,0:T(8,128)}, f32[4,1,1]{0,2,1:T(1,128)S(1)}, f32[4,1,12,1,1]{2,4...) while((s32[]{:T(128)}, ...), condition=%wide.region_4.5_spmd.clone, body=%wide.region_3.4_spmd.clone.sunk | while | flops 393243 | bytes 3935500 | solution.py:76
  237.7 2.4 copy.416
  240.2 2.8 fusion.147
  243.1 17.6 %fusion.28 = f32[1,4,256,12,64]{2,4,3,1,0:T(8,128)S(1)} fusion(f32[4,256,12,64]{1,3,2,0:T(8,128)S(1)} %bitcast.334, f32[1,4,256,12,64]{2,1,4,3,0:T(4,128)} %reshape.869, f32[12]{0:T(128)S(1)} %copy-done.79, f32[4,256,12]{1,2,0:T(8,128)S(1)} %copy.418, f32[4,256,256]{2,1,0:T(8,128)S(1)} %copy-done.24, f32[4,256,256]{2,1,0:T(8,128)S(1)} %copy-done.22, ...), kind=kOutput, calls=%fused_computation.59 | convolution fusion | flops 2432434176 | bytes 15089712 | tf_op jit(solution)/shard_map/jvp(vmap(bhts,bshp->bthp))/dot_general | solution.py:60
  260.7 2.0 copy.421
  262.7 2.4 copy.478
  265.2 3.5 copy.422
  268.7 5.4 multiply_reduce_fusion.9
  274.1 11.6 %psum.77 = f32[1024]{0:T(1024)S(1)} all-reduce(f32[1024]{0:T(1024)S(1)} %get-tuple-element.565), channel_id=1, replica_groups=mesh['dp'=8,'tensor'=4] {'tensor'}, use_global_device_ids=true, to_apply=%region_6.7 | all-reduce | flops 1024 | bytes 8192 | tf_op jit(solution)/shard_map/psum | solution.py:167
  285.8 8.6 %multiply_reduce_fusion.1 = (f32[768]{0:T(1024)}, f32[1024]{0:T(1024)S(1)}, f32[1024,768]{1,0:T(8,128)}) fusion(f32[1024,768]{1,0:T(8,128)} %get-tuple-element.566, f32[1024]{0:T(1024)S(1)} %get-tuple-element.596, f32[768]{0:T(1024)S(1)} %copy-done.69, bf16[1024,1536]{1,0:T(8,128)(2,1)} %all-gather.12.cloned.1.call-done, ...), kind=kOutput, calls=%fused_computation.76 | convolution fusion | flops 2420635904 | bytes 11810816 | tf_op jit(solution)/shard_map/td,cd->tc/dot_general | solution.py:181
  294.4 8.3 psum.78
  302.7 8.9 %fusion.29 = (f32[768]{0:T(1024)}, f32[1024,768]{1,0:T(8,128)}, bf16[1024,1,768]{2,0,1:T(8,128)(2,1)}) fusion(f32[1,1024,768]{2,1,0:T(8,128)} %get-tuple-element.570, f32[1024,1536]{1,0:T(8,128)} %copy-done.2, f32[1024]{0:T(1024)S(1)} %psum.78, f32[1024,768]{1,0:T(8,128)} %get-tuple-element.566, f32[1024]{0:T(1024)S(1)} %get-tuple-element.595, ...), kind=kLoop, calls=%fused_computation.61 | loop fusion | flops 18873600 | bytes 20465664 | tf_op jit(solution)/shard_map/transpose(jvp(vmap()))/reduce_sum | solution.py:87
  311.6 3.6 copy.424
  315.2 5.2 reshape.872
  320.4 5.3 reshape.871
  325.7 4.5 multiply_reduce_fusion.6
  330.4 10.9 %fusion.82 = f32[4,256,128]{2,1,0:T(8,128)} fusion(f32[4,256,12,64]{1,0,3,2:T(4,128)S(1)} %copy-done.1, f32[4,256,12]{1,2,0:T(8,128)S(1)} %copy.418, f32[4,1,12,128,64]{4,3,2,1,0:T(8,128)S(1)} %copy-done), kind=kOutput, calls=%fused_computation.135 | convolution fusion | flops 1208745984 | bytes 5292032 | tf_op jit(solution)/shard_map/transpose(jvp(vmap(btn,bhnp->bthp)))/dot_general | solution.py:85
  341.3 4.5 fusion.76
  345.8 2.0 broadcast.354
  347.8 22.1 %while.37 = (s32[]{:T(128)}, f32[1,12,128,64]{3,2,1,0:T(8,128)S(1)}, f32[4,1,12,128,64]{4,3,2,1,0:T(8,128)}, f32[4,1,12]{2,1,0:T(1,128)S(1)}, f32[4,1,12,128,64]...) while((s32[]{:T(128)}, ...), condition=%wide.region_12.13_spmd.clone, body=%wide.region_10.12_spmd.clone.sunk | while | flops 589828 | bytes 4326768 | solution.py:76
  370.7 23.0 %fusion.11 = (f32[4,12,256]{2,1,0:T(8,128)}, f32[4,12,256]{2,1,0:T(8,128)}, f32[4,256,256]{2,1,0:T(8,128)S(1)}) fusion(f32[4,256,256]{2,1,0:T(8,128)} %fusion.146, f32[4,256,256]{2,1,0:T(8,128)} %get-tuple-element.592, f32[4,12,256]{2,1,0:T(8,128)S(1)} %copy-done.39, pred[4,256,256]{2,1,0:T(8,128)(4,1)S(1)} %copy-done.34, f32[4,256,12,64]{1,0,3,2:T(4,128)} %reshape.855, ...), kind=kOutput, calls=%fused_computation.25 | convolution fusion | flops 2451021824 | bytes 9895936 | tf_op jit(solution)/shard_map/transpose(jvp(vmap(bhts,bshp->bthp)))/dot_general | solution.py:60
  394.8 5.1 fusion.33
  400.0 3.3 fusion.88
  403.5 14.2 %fusion.35 = (f32[4,256,12]{1,2,0:T(8,128)S(1)}, f32[4,256,12]{1,2,0:T(8,128)}, f32[1,4,256,12,64]{2,4,3,1,0:T(8,128)}) fusion(f32[4,12,64,256]{3,2,1,0:T(8,128)S(1)} %fusion.33, f32[1,4,256,12,64]{2,1,4,3,0:T(4,128)S(1)} %copy-done.17, f32[4,256,12]{1,2,0:T(8,128)S(1)} %copy.397, f32[1,4,256,12,64]{2,1,4,3,0:T(4,128)S(1)} %copy-done.18, ...), kind=kOutput, calls=%fused_computation.69 | convolution fusion | flops 2436341760 | bytes 18333744 | tf_op jit(solution)/shard_map/transpose(jvp(vmap(bhts,bshp->bthp)))/dot_general | solution.py:60
  419.7 2.2 pad_add_fusion.3
  424.8 9.9 %reduce-window.16 = f32[1,4,12,2,128]{4,2,3,1,0:T(8,128)S(1)} reduce-window(f32[1,4,12,2,128]{4,2,3,1,0:T(8,128)S(1)} %copy.447, f32[]{:T(128)} %constant.112.clone.1), window={size=1x1x1x1x128 pad=0_0x0_0x0_0x0_0x0_127}, to_apply=%region_19.20 | reduce-window | flops 1560576 | bytes 98308 | tf_op jit(solution)/shard_map/reduce-window.2
  438.1 7.0 convolution_convert_fusion.2
  445.2 5.7 copy.433
  450.9 5.5 reshape.875
  456.5 3.6 copy.434
  460.1 8.6 %multiply_reduce_fusion.5 = (f32[768]{0:T(1024)S(1)}, f32[768]{0:T(1024)S(1)}, f32[768]{0:T(1024)S(1)}, f32[768]{0:T(1024)S(1)}, f32[768]{0:T(1024)S(1)}, /*index=5*/f32[1,1024,768]{2,1,0:T(8,128)S(1)}) fusion(f32[1,1024,768]{2,1,0:T(8,128)} %copy-done.7, f32[1024]{0:T(1024)S(1)} %bitcast.363, f32[1024]{0:T(1024)S(1)} %bitcast.357, f32[1024]{0:T(1024)S(1)} %bitcast.351, ...), kind=kLoop, calls=%fused_computation.80 | loop fusion | flops 16511232 | bytes 15756288 | tf_op jit(solution)/shard_map/transpose(jvp(vmap()))/reduce_sum | solution.py:32
  471.4 5.1 fusion.49
  476.4 2.8 fusion.12
  479.3 6.9 convolution_convert_fusion.1
  486.3 8.9 %convolution_convert_fusion = bf16[1536,2,768]{2,0,1:T(8,128)(2,1)} fusion(bf16[1024,1536]{1,0:T(8,128)(2,1)S(1)} %copy-done.5, bf16[1024,1,768]{2,0,1:T(8,128)(2,1)} %copy-done.21, bf16[1024,1,768]{2,0,1:T(8,128)(2,1)} %get-tuple-element.575), kind=kOutput, calls=%fused_computation.41 | convolution fusion | flops 4840488960 | bytes 11010048 | tf_op jit(solution)/shard_map/td,tkc->dkc/dot_general | solution.py:207
  496.8 2.3 multiply_reduce_fusion.13
  502.6 6.9 reduce-scatter.19.cloned.1.call-done
  511.0 23.2 %all-reduce.25 = (f32[4,768]{1,0:T(4,128)}, f32[768]{0:T(1024)}, f32[4,256]{1,0:T(4,128)}, f32[256]{0:T(256)}, f32[12]{0:T(128)}, /*index=5*/f32[12]{0:T(128)}, f32[12]{0:T(128)}, f32[768]{0:T(1024)}) all-reduce(f32[4,768]{1,0:T(4,128)S(1)} %pad_add_fusion.4, ...), channel_id=1, replica_groups=mesh['dp'=8,'tensor'=4] {'dp'}, use_global_device_ids=true, to_apply=%region_34.35 | all-reduce | flops 5924 | bytes 47392 | tf_op jit(solution)/shard_map/psum | solution.py:230
  534.2 21.0 %reduce-scatter.17.cloned.1.call-done = bf16[768,192]{0,1:T(8,128)(2,1)} async-done(((bf16[768,1536]{0,1:T(8,128)(2,1)}), bf16[768,192]{0,1:T(8,128)(2,1)}) %reduce-scatter.17.cloned.1.call-update) | async-done | bytes 294928 | tf_op jit(solution)/shard_map/reduce_scatter | solution.py:222
  557.0 60.9 %reduce-scatter.11.cloned.1.call-done = bf16[256,1536]{1,0:T(8,128)(2,1)} async-done(((bf16[1024,1536]{1,0:T(8,128)(2,1)}), bf16[256,1536]{1,0:T(8,128)(2,1)}) %reduce-scatter.11.cloned.1.call-update) | async-done | bytes 786448 | tf_op jit(solution)/shard_map/reduce_scatter | solution.py:199
  618.0 2.1 fusion.65
  620.1 44.7 %all-reduce.24 = f32[1536]{0:T(1024)S(1)} all-reduce(f32[1536]{0:T(1024)S(1)} %get-tuple-element.508), channel_id=4, replica_groups=mesh['dp'=8,'tensor'=4] {'dp','tensor'}, use_global_device_ids=true, to_apply=%region_26.27.clone | all-reduce | flops 1536 | bytes 12288
  665.3 16.4 %reduce-scatter.9.cloned.1.call-done = bf16[256,1536]{1,0:T(8,128)(2,1)} async-done(((bf16[1024,1536]{1,0:T(8,128)(2,1)}), bf16[256,1536]{1,0:T(8,128)(2,1)}) %reduce-scatter.9.cloned.1.call-update) | async-done | bytes 786448 | tf_op jit(solution)/shard_map/reduce_scatter | solution.py:171
  681.7 3.1 fusion.61
  684.8 53.8 %reduce-scatter.13.cloned.1.call-done = bf16[192,2,768]{2,0,1:T(8,128)(2,1)} async-done(((bf16[1536,2,768]{2,0,1:T(8,128)(2,1)}), bf16[192,2,768]{2,0,1:T(8,128)(2,1)}) %reduce-scatter.13.cloned.1.call-update) | async-done | bytes 589840 | tf_op jit(solution)/shard_map/reduce_scatter | solution.py:216
  738.6 2.7 copy.458
  741.3 101.0 %reduce-scatter.15.cloned.1.call-done = f32[48,256]{1,0:T(8,128)} async-done(((f32[1536,256]{1,0:T(8,128)}), f32[48,256]{1,0:T(8,128)}) %reduce-scatter.15.cloned.1.call-update) | async-done | bytes 49168 | tf_op jit(solution)/shard_map/reduce_scatter | solution.py:227
  (404 shorter events, 80.9 us)
Async XLA Ops:
  7.2 48.0 %copy-start.27 = (bf16[192,2,768]{2,1,0:T(2,128)(2,1)S(1)}, bf16[192,2,768]{2,1,0:T(2,128)(2,1)}, u32[]{:S(2)}) copy-start(bf16[192,2,768]{2,1,0:T(2,128)(2,1)} %param.24) | copy-start | bytes 1769476
  7.2 50.3 %copy-start.81 = (f32[12]{0:T(128)S(1)}, f32[12]{0:T(128)}, u32[]{:S(2)}) copy-start(f32[12]{0:T(128)} %param.32) | copy-start | bytes 148
  7.2 50.3 %copy-start.49 = (s32[1,1024]{1,0:T(1,128)S(1)}, s32[1,1024]{1,0:T(1,128)}, u32[]{:S(2)}) copy-start(s32[1,1024]{1,0:T(1,128)} %param.21) | copy-start | bytes 12292
  7.2 51.8 %copy-start.72 = (f32[4,256]{1,0:T(4,128)S(1)}, f32[4,256]{1,0:T(4,128)}, u32[]{:S(2)}) copy-start(f32[4,256]{1,0:T(4,128)} %param.29) | copy-start | bytes 12292
  7.2 51.8 %copy-start.56 = (f32[4,768]{1,0:T(4,128)S(1)}, f32[4,768]{1,0:T(4,128)}, u32[]{:S(2)}) copy-start(f32[4,768]{1,0:T(4,128)} %param.27) | copy-start | bytes 36868
  7.2 52.0 %copy-start.67 = (bf16[192,12]{0,1:T(8,128)(2,1)S(1)}, bf16[192,12]{0,1:T(8,128)(2,1)}, u32[]{:S(2)}) copy-start(bf16[192,12]{0,1:T(8,128)(2,1)} %param.26) | copy-start | bytes 13828
  7.2 147.3 %all-gather.6.cloned.1.call-start = ((), (), s32[]{:S(2)}) async-start(), calls=%async_computation.6 | async-start | bytes 3932160 | tf_op jit(solution)/shard_map/all_gather | solution.py:127
  7.3 62.0 %copy-start.52 = (bf16[48,256]{1,0:T(8,128)(2,1)S(1)}, bf16[48,256]{1,0:T(8,128)(2,1)}, u32[]{:S(2)}) copy-start(bf16[48,256]{1,0:T(8,128)(2,1)} %param.25) | copy-start | bytes 73732
  9.3 49.8 %copy-start.65 = (f32[256]{0:T(256)}, f32[256]{0:T(256)S(1)}, u32[]{:S(2)}) copy-start(f32[256]{0:T(256)S(1)} %get-tuple-element.607) | copy-start | bytes 3076
  55.1 99.4 %copy-start.75 = (f32[12]{0:T(128)S(1)}, f32[12]{0:T(128)}, u32[]{:S(2)}) copy-start(f32[12]{0:T(128)} %param.31) | copy-start | bytes 148
  55.1 115.2 %all-gather.8.cloned.1.call-start = ((), (), s32[]{:S(2)}) async-start(), calls=%async_computation.7 | async-start | bytes 5308416 | tf_op jit(solution)/shard_map/all_gather | solution.py:117
  56.1 229.7 %all-gather.10.cloned.1.call-start = ((), (), s32[]{:S(2)}) async-start(), calls=%async_computation.8 | async-start | bytes 2654208 | tf_op jit(solution)/shard_map/all_gather | solution.py:119
  56.8 229.0 %all-gather.12.cloned.1.call-start = ((), (), s32[]{:S(2)}) async-start(), calls=%async_computation.10 | async-start | bytes 3932160 | tf_op jit(solution)/shard_map/all_gather | solution.py:180
  57.4 438.0 %all-reduce.28.cloned.1.call-start = ((), (), s32[]{:S(2)}) async-start(), calls=%async_computation.12 | async-start | bytes 2097152 | tf_op jit(solution)/shard_map/psum | solution.py:192
  57.6 100.5 %copy-start.74 = (f32[12]{0:T(128)}, f32[12]{0:T(128)S(1)}, u32[]{:S(2)}) copy-start(f32[12]{0:T(128)S(1)} %exponential_negate_fusion) | copy-start | bytes 148
  59.1 106.6 %copy-start.57 = (f32[1,256]{1,0:T(1,128)}, f32[1,256]{1,0:T(1,128)S(1)}, u32[]{:S(2)}) copy-start(f32[1,256]{1,0:T(1,128)S(1)} %get-tuple-element.599) | copy-start | bytes 3076
  59.1 106.6 %copy-start.59 = (f32[1,256]{1,0:T(1,128)}, f32[1,256]{1,0:T(1,128)S(1)}, u32[]{:S(2)}) copy-start(f32[1,256]{1,0:T(1,128)S(1)} %get-tuple-element.600) | copy-start | bytes 3076
  59.1 106.6 %copy-start.61 = (f32[1,256]{1,0:T(1,128)}, f32[1,256]{1,0:T(1,128)S(1)}, u32[]{:S(2)}) copy-start(f32[1,256]{1,0:T(1,128)S(1)} %get-tuple-element.601) | copy-start | bytes 3076
  59.1 106.6 %copy-start.63 = (f32[1,256]{1,0:T(1,128)}, f32[1,256]{1,0:T(1,128)S(1)}, u32[]{:S(2)}) copy-start(f32[1,256]{1,0:T(1,128)S(1)} %get-tuple-element.602) | copy-start | bytes 3076
  59.1 126.2 %copy-start.41 = (f32[768]{0:T(1024)}, f32[768]{0:T(1024)S(1)}, u32[]{:S(2)}) copy-start(f32[768]{0:T(1024)S(1)} %get-tuple-element.516) | copy-start | bytes 9220
  59.2 126.2 %copy-start.43 = (f32[768]{0:T(1024)}, f32[768]{0:T(1024)S(1)}, u32[]{:S(2)}) copy-start(f32[768]{0:T(1024)S(1)} %get-tuple-element.517) | copy-start | bytes 9220
  59.2 126.2 %copy-start.45 = (f32[768]{0:T(1024)}, f32[768]{0:T(1024)S(1)}, u32[]{:S(2)}) copy-start(f32[768]{0:T(1024)S(1)} %get-tuple-element.518) | copy-start | bytes 9220
  69.4 88.6 %copy-start.28 = (bf16[1536,12]{0,1:T(8,128)(2,1)}, bf16[1536,12]{0,1:T(8,128)(2,1)S(1)}, u32[]{:S(2)}) copy-start(bf16[1536,12]{0,1:T(8,128)(2,1)S(1)} %reshape.896) | copy-start | bytes 110596
  152.9 9.7 %copy-start.26 = (bf16[1536,256]{1,0:T(8,128)(2,1)}, bf16[1536,256]{1,0:T(8,128)(2,1)S(1)}, u32[]{:S(2)}) copy-start(bf16[1536,256]{1,0:T(8,128)(2,1)S(1)} %all_gather.28) | copy-start | bytes 2359300
  154.5 6.9 copy-start.47
  158.0 7.6 copy-start.30
  167.6 38.3 %copy-start.10 = (f32[1,1024,128]{2,1,0:T(8,128)}, f32[1,1024,128]{2,1,0:T(8,128)S(1)}, u32[]{:S(2)}) copy-start(f32[1,1024,128]{2,1,0:T(8,128)S(1)} %get-tuple-element.585) | copy-start | bytes 1572868
  185.3 6.7 copy-start.7
  237.7 5.3 copy-start.34
  237.7 5.3 copy-start.39
  243.0 17.7 %copy-start.12 = (f32[4,256,768]{1,2,0}, f32[4,256,768]{1,2,0:S(1)}, u32[]{:S(2)}) copy-start(f32[4,256,768]{1,2,0:S(1)} %fusion.147) | copy-start | bytes 9437188
  268.7 17.1 %copy-start.69 = (f32[768]{0:T(1024)S(1)}, f32[768]{0:T(1024)}, u32[]{:S(2)}) copy-start(f32[768]{0:T(1024)} %param.34) | copy-start | bytes 9220
  285.7 17.0 %copy-start.54 = (f32[1024]{0:T(1024)}, f32[1024]{0:T(1024)S(1)}, u32[]{:S(2)}) copy-start(f32[1024]{0:T(1024)S(1)} %get-tuple-element.596) | copy-start | bytes 12292
  325.7 4.7 copy-start.1
  341.2 6.5 copy-start.86
  370.7 24.1 %copy-start.6 = (f32[4,1,12,128,64]{4,3,2,1,0:T(8,128)S(1)}, f32[4,1,12,128,64]{4,3,2,1,0:T(8,128)}, u32[]{:S(2)}) copy-start(f32[4,1,12,128,64]{4,3,2,1,0:T(8,128)} %get-tuple-element.223) | copy-start | bytes 4718596
  370.7 24.1 %copy-start.11 = (f32[1,1024,128]{2,1,0:T(8,128)S(1)}, f32[1,1024,128]{2,1,0:T(8,128)}, u32[]{:S(2)}) copy-start(f32[1,1024,128]{2,1,0:T(8,128)} %copy-done.10) | copy-start | bytes 1572868
  394.8 5.2 copy-start.4
  394.8 8.6 %copy-start.25 = (f32[4,256,256]{2,1,0:T(8,128)S(1)}, f32[4,256,256]{2,1,0:T(8,128)}, u32[]{:S(2)}) copy-start(f32[4,256,256]{2,1,0:T(8,128)} %fusion.146) | copy-start | bytes 3145732
  394.8 8.6 %copy-start.35 = (pred[4,256,256]{2,1,0:T(8,128)(4,1)S(1)}, pred[4,256,256]{2,1,0:T(8,128)(4,1)}, u32[]{:S(2)}) copy-start(pred[4,256,256]{2,1,0:T(8,128)(4,1)} %get-tuple-element.591) | copy-start | bytes 786436
  403.4 15.2 %copy-start.19 = (f32[4,256,128]{2,1,0:T(8,128)S(1)}, f32[4,256,128]{2,1,0:T(8,128)}, u32[]{:S(2)}) copy-start(f32[4,256,128]{2,1,0:T(8,128)} %fusion.82) | copy-start | bytes 1572868
  418.6 5.2 copy-start.33
  418.6 5.2 copy-start.48
  418.6 16.6 %copy-start.31 = (f32[1,4,256,12]{2,1,3,0:T(4,128)S(1)}, f32[1,4,256,12]{2,1,3,0:T(4,128)}, u32[]{:S(2)}) copy-start(f32[1,4,256,12]{2,1,3,0:T(4,128)} %copy-done.30) | copy-start | bytes 147460
  419.7 16.6 %copy-start.32 = (f32[1024,12]{0,1:T(8,128)S(1)}, f32[1024,12]{0,1:T(8,128)}, u32[]{:S(2)}) copy-start(f32[1024,12]{0,1:T(8,128)} %get-tuple-element.611) | copy-start | bytes 147460
  419.7 16.8 %copy-start.5 = (bf16[1024,1536]{1,0:T(8,128)(2,1)S(1)}, bf16[1024,1536]{1,0:T(8,128)(2,1)}, u32[]{:S(2)}) copy-start(bf16[1024,1536]{1,0:T(8,128)(2,1)} %all-gather.6.cloned.1.call-done) | copy-start | bytes 9437188
  422.0 87.5 %reduce-scatter.19.cloned.1.call-start = ((), (), s32[]{:S(2)}) async-start(), calls=%async_computation.16 | async-start | bytes 442368
  438.0 117.2 %reduce-scatter.17.cloned.1.call-start = ((), (), s32[]{:S(2)}) async-start(), calls=%async_computation.15 | async-start | bytes 2654208 | tf_op jit(solution)/shard_map/reduce_scatter | solution.py:222
  445.2 172.8 %reduce-scatter.11.cloned.1.call-start = ((), (), s32[]{:S(2)}) async-start(), calls=%async_computation.11 | async-start | bytes 3932160 | tf_op jit(solution)/shard_map/reduce_scatter | solution.py:199
  460.1 8.6 %copy-start.42 = (f32[768]{0:T(1024)S(1)}, f32[768]{0:T(1024)}, u32[]{:S(2)}) copy-start(f32[768]{0:T(1024)} %copy-done.41) | copy-start | bytes 9220
  460.1 8.7 %copy-start.44 = (f32[768]{0:T(1024)S(1)}, f32[768]{0:T(1024)}, u32[]{:S(2)}) copy-start(f32[768]{0:T(1024)} %copy-done.43) | copy-start | bytes 9220
  460.1 8.7 %copy-start.46 = (f32[768]{0:T(1024)S(1)}, f32[768]{0:T(1024)}, u32[]{:S(2)}) copy-start(f32[768]{0:T(1024)} %copy-done.45) | copy-start | bytes 9220
  460.1 10.8 %slice-start = ((s8[4718592]{0:T(1024)(128)(4,1)}), s8[4194304]{0:T(1024)(128)(4,1)S(1)}, s32[]{:S(2)}) async-start(s8[4718592]{0:T(1024)(128)(4,1)} %bitcast.339), calls=%async_computation.17 | async-start | bytes 8388608
  470.9 5.5 copy-start.21
  471.4 5.1 copy-start.29
  479.2 202.4 %reduce-scatter.9.cloned.1.call-start = ((), (), s32[]{:S(2)}) async-start(), calls=%async_computation.9 | async-start | bytes 3932160 | tf_op jit(solution)/shard_map/reduce_scatter | solution.py:171
  486.2 252.4 %reduce-scatter.13.cloned.1.call-start = ((), (), s32[]{:S(2)}) async-start(), calls=%async_computation.13 | async-start | bytes 5308416 | tf_op jit(solution)/shard_map/reduce_scatter | solution.py:216
  495.3 347.1 %reduce-scatter.15.cloned.1.call-start = ((), (), s32[]{:S(2)}) async-start(), calls=%async_computation.14 | async-start | bytes 1622016 | tf_op jit(solution)/shard_map/reduce_scatter | solution.py:227
  500.7 10.3 %copy-start.73 = (f32[768]{0:T(1024)S(1)}, f32[768]{0:T(1024)}, u32[]{:S(2)}) copy-start(f32[768]{0:T(1024)} %get-tuple-element.499) | copy-start | bytes 9220
  500.7 117.2 %copy-start.13 = (bf16[256,1536]{1,0:T(8,128)(2,1)S(1)}, bf16[256,1536]{1,0:T(8,128)(2,1)}, u32[]{:S(2)}) copy-start(bf16[256,1536]{1,0:T(8,128)(2,1)} %param.20) | copy-start | bytes 2359300
  500.7 117.2 %copy-start.37 = (f32[1536]{0:T(1024)S(1)}, f32[1536]{0:T(1024)}, u32[]{:S(2)}) copy-start(f32[1536]{0:T(1024)} %copy-done.36) | copy-start | bytes 18436
  500.7 117.2 %copy-start.66 = (f32[256]{0:T(256)S(1)}, f32[256]{0:T(256)}, u32[]{:S(2)}) copy-start(f32[256]{0:T(256)} %copy-done.65) | copy-start | bytes 3076
  502.3 179.3 %copy-start.16 = (bf16[256,1536]{1,0:T(8,128)(2,1)S(1)}, bf16[256,1536]{1,0:T(8,128)(2,1)}, u32[]{:S(2)}) copy-start(bf16[256,1536]{1,0:T(8,128)(2,1)} %param.22) | copy-start | bytes 2359300
  502.3 179.3 %copy-start.71 = (f32[256]{0:T(256)S(1)}, f32[256]{0:T(256)}, u32[]{:S(2)}) copy-start(f32[256]{0:T(256)} %get-tuple-element.606) | copy-start | bytes 3076
  (54 other events, 114.6 us)
Sparse Core Ops, SparseCore 0:
  55.2 74.6 all-gather.5
  132.4 37.9 all-gather.7
  172.3 28.8 all-gather.9
  202.6 63.4 all-gather.11
  422.1 50.6 all-reduce.27
  476.3 33.1 reduce-scatter.18
  512.8 42.3 reduce-scatter.16
  557.5 60.3 reduce-scatter.10
  620.3 61.3 reduce-scatter.8
  685.0 53.6 reduce-scatter.12
  744.4 97.8 reduce-scatter.14
where the time goes:
time: 855 us; the launch traced here: 849 us
  waiting for transfers between devices  262 us (31%)
  blocking collectives  223 us (26%)
  matrix products  150 us (18%)
  local copies, waits for them, and re-layouts  103 us (12%)
  other arithmetic  93.6 us (11%)
  between operations  15.6 us (2%)
    reduce_scatter x1, waiting for transfers between devices, body(): lax.psum_scatter(g_bc, ('dp', 'tensor'), scatter_dimension=0, tiled=True)  101 us
    unnamed x2, blocking collectives  86.7 us
    all_gather x1, blocking collectives, body(): lax.all_gather(w_bc, ('dp', 'tensor'), axis=0, tiled=True)  83.5 us
    reduce_scatter x1, waiting for transfers between devices, body(): lax.psum_scatter(input_part.astype(jnp.bfloat16), 'tensor', scatter_dimen...  60.9 us
    dot_general x3, matrix products, mixer_sequence(): jnp.einsum('bhts,bshp->bthp', decay * scores[:, None], weighted, precisio...  54.7 us
    reduce_scatter x1, waiting for transfers between devices, body(): lax.psum_scatter(g_zx.astype(jnp.bfloat16), 'dp', scatter_dimension=0, ti...  53.8 us
    psum x1, blocking collectives, body(): lax.psum((g_cxw, g_cxb, g_dtb, g_alog, g_skip, g_gate_gain, g_cbw, g_cbb)...  23.2 us
    reduce_scatter x1, waiting for transfers between devices, body(): lax.psum_scatter(g_out.astype(jnp.bfloat16), 'dp', scatter_dimension=1, t...  21 us
  transfers between devices with their start and end apart: 11, of which 7 were waited for; matrix products, arithmetic and copies ran while one was open for 24% of the time, Pallas kernels for 0%

commit v1 on v0

v1 whole, which is shorter than its diff:
```python
import functools
import jax
import jax.numpy as jnp
from jax import lax
from jax.experimental import pallas as pl
from jax.experimental.pallas import tpu as pltpu
from jax.sharding import PartitionSpec as P

HEAD_DIM = 64
STATE = 128
CHUNK = 128
LANES = 128
HALO = 8
HIGHEST = lax.Precision.HIGHEST
NEGATIVE = -1e30
F32 = jnp.float32
BF16 = jnp.bfloat16


def mm(a, b, dims=((1,), (0,))):
    return lax.dot_general(a, b, (dims, ((), ())), preferred_element_type=F32)


def mm_exact(a, b, dims=((1,), (0,))):
    return lax.dot_general(a, b, (dims, ((), ())), precision=HIGHEST, preferred_element_type=F32)


NT = ((1,), (1,))
TN = ((0,), (0,))


def spread(per_head, expand):
    high = per_head.astype(BF16)
    rest = per_head - high.astype(F32)
    middle = rest.astype(BF16)
    low = (rest - middle.astype(F32)).astype(BF16)
    return mm(high, expand) + (mm(middle, expand) + mm(low, expand))


def gather_heads(values, expand):
    high = values.astype(BF16)
    low = (values - high.astype(F32)).astype(BF16)
    return mm(high, expand, NT) + mm(low, expand, NT)


def head_expand(width):
    rows = lax.broadcasted_iota(jnp.int32, (LANES, width), 0)
    columns = lax.broadcasted_iota(jnp.int32, (LANES, width), 1)
    lower = rows * HEAD_DIM
    return ((columns >= lower) & (columns < lower + HEAD_DIM)).astype(F32).astype(BF16)


def triangle(size):
    rows = lax.broadcasted_iota(jnp.int32, (size, size), 0)
    columns = lax.broadcasted_iota(jnp.int32, (size, size), 1)
    return rows >= columns


def sigmoid(values):
    return 1.0 / (1.0 + jnp.exp(-values))


def softplus(values):
    return jnp.maximum(values, 0.0) + jnp.log(1.0 + jnp.exp(-jnp.abs(values)))


def conv_chunk(window, meta, taps, offset):
    total = offset + taps[0:1] * window[pl.ds(HALO, CHUNK), :]
    for back in (1, 2, 3):
        total = total + taps[back : back + 1] * (
            window[pl.ds(HALO - back, CHUNK), :] * meta[:, back : back + 1]
        )
    return total


def split_pair(values):
    lane = lax.broadcasted_iota(jnp.int32, values.shape, 1)
    zero = jnp.zeros_like(values)
    return jnp.where(lane < HEAD_DIM, values, zero), jnp.where(lane < HEAD_DIM, zero, values)


def decays(dt_pre, heads, meta, lower):
    step = softplus(dt_pre + heads[5:6, :LANES])
    rate = step * heads[6:7, :LANES]
    cumulative = mm_exact(lower, rate)
    return step, cumulative


def forward_kernel(
    gate_ref, conv_ref, bc_ref, dt_ref, meta_ref, seg_row_ref, params_ref,
    core_ref, gated_ref, states_ref, sum_ref, pre_ref, lanes_ref, save_ref,
    window, state,
):
    width = conv_ref.shape[1]
    chunk = pl.program_id(0)

    @pl.when(chunk == 0)
    def _():
        window[pl.ds(0, HALO), :] = jnp.zeros((HALO, window.shape[1]), F32)
        state[...] = jnp.zeros_like(state)

    @pl.when(chunk > 0)
    def _():
        window[pl.ds(0, HALO), :] = window[pl.ds(CHUNK, HALO), :]

    window[pl.ds(HALO, CHUNK), :width] = conv_ref[...]
    window[pl.ds(HALO, CHUNK), width:] = bc_ref[...]
    meta = meta_ref[...]
    pre = conv_chunk(window, meta, params_ref, params_ref[4:5])
    pre_ref[...] = pre
    act = pre * sigmoid(pre)
    mixer_in = act[:, :width]
    input_mat = act[:, width : width + STATE].astype(BF16)
    output_mat = act[:, width + STATE :].astype(BF16)
    below = triangle(CHUNK)
    lower = below.astype(F32)
    visible = below & (meta[:, 5:6] == seg_row_ref[0])
    step, cumulative = decays(dt_ref[...], params_ref, meta, lower)
    cum_rows = cumulative.T
    last = cumulative[CHUNK - 1 : CHUNK]
    expand = head_expand(width)
    step_l = spread(step, expand)
    from_prev_l = spread(jnp.exp(cumulative) * meta[:, 0:1], expand)
    to_end_l = spread(jnp.exp(last - cumulative) * meta[:, 4:5], expand)
    lanes_ref[:, :width] = step_l
    lanes_ref[:, width : 2 * width] = from_prev_l
    lanes_ref[:, 2 * width :] = to_end_l
    save_ref[:, :LANES] = step
    save_ref[:, LANES:] = cumulative
    passing = from_prev_l[CHUNK - 1 : CHUNK]
    weighted = mixer_in * step_l
    weighted_b = weighted.astype(BF16)
    scores = mm(output_mat, input_mat, NT)
    incoming = state[...]
    incoming_b = incoming.astype(BF16)
    states_ref[0] = incoming_b
    before = mm(output_mat, incoming_b) * from_prev_l
    skipped = params_ref[7:8, :width] * mixer_in
    for pair in range(width // LANES):
        mixed = []
        for head in (2 * pair, 2 * pair + 1):
            gap = cumulative[:, head : head + 1] - cum_rows[head : head + 1, :]
            decay = jnp.exp(jnp.where(visible, gap, NEGATIVE))
            mixed.append((decay * scores).astype(BF16))
        first, second = split_pair(weighted_b[:, pair * LANES : (pair + 1) * LANES])
        within = mm(jnp.concatenate(mixed, 1), jnp.concatenate([first, second], 0))
        lanes = slice(pair * LANES, (pair + 1) * LANES)
        core_ref[:, lanes] = within + before[:, lanes] + skipped[:, lanes]
    state[...] = passing * incoming + mm(input_mat, (weighted * to_end_l).astype(BF16), TN)
    gate = gate_ref[...]
    gated = core_ref[...] * (gate * sigmoid(gate))
    gated_ref[...] = gated
    square = gated * gated
    sum_ref[...] = mm_exact(jnp.ones((8, width), F32), square, NT)


def ssm_forward(projected, bc_pre, meta, seg_row, params):
    length, width = projected.shape[0], params.shape[1] - 2 * STATE
    chunks = length // CHUNK
    row = lambda n, at=0: pl.BlockSpec((CHUNK, n), lambda c: (c, at))
    fixed = lambda a: pl.BlockSpec(a.shape, lambda c: (0,) * a.ndim)
    return pl.pallas_call(
        forward_kernel,
        grid=(chunks,),
        in_specs=[
            row(width), row(width, 1), row(2 * STATE), row(LANES, 2 * width // LANES), row(8),
            pl.BlockSpec((1, 1, CHUNK), lambda c: (c, 0, 0)),
            fixed(params),
        ],
        out_specs=[
            row(width), row(width),
            pl.BlockSpec((1, STATE, width), lambda c: (c, 0, 0)),
            pl.BlockSpec((8, CHUNK), lambda c: (0, c)),
            row(width + 2 * STATE), row(3 * width), row(2 * LANES),
        ],
        out_shape=[
            jax.ShapeDtypeStruct((length, width), F32),
            jax.ShapeDtypeStruct((length, width), F32),
            jax.ShapeDtypeStruct((chunks, STATE, width), BF16),
            jax.ShapeDtypeStruct((8, length), F32),
            jax.ShapeDtypeStruct((length, width + 2 * STATE), F32),
            jax.ShapeDtypeStruct((length, 3 * width), F32),
            jax.ShapeDtypeStruct((length, 2 * LANES), F32),
        ],
        scratch_shapes=[
            pltpu.VMEM((CHUNK + HALO, width + 2 * STATE), F32),
            pltpu.VMEM((STATE, width), F32),
        ],
        name="ssm_forward",
    )(projected, projected, bc_pre, projected, meta, seg_row, params)


def backward_kernel(
    inner,
    gate_ref, conv_ref, halo_ref, bc_ref, bc_halo_ref, dt_ref, meta_ref, meta_next_ref, seg_row_ref,
    params_ref, core_ref, d_normed_ref, rms_ref, dots_ref, states_ref, pre_ref, lanes_ref, save_ref,
    dz_ref, dbc_ref, gconv_ref, ghead_ref, ggain_ref, gskip_ref,
    window, d_window, d_state,
):
    width = conv_ref.shape[1]
    place = pl.program_id(0)
    chunk = pl.num_programs(0) - 1 - place

    @pl.when(place == 0)
    def _():
        d_window[pl.ds(CHUNK, HALO), :] = jnp.zeros((HALO, d_window.shape[1]), F32)
        d_state[...] = jnp.zeros_like(d_state)
        gconv_ref[...] = jnp.zeros_like(gconv_ref)
        ghead_ref[...] = jnp.zeros_like(ghead_ref)
        ggain_ref[...] = jnp.zeros_like(ggain_ref)
        gskip_ref[...] = jnp.zeros_like(gskip_ref)

    @pl.when(place > 0)
    def _():
        d_window[pl.ds(CHUNK, HALO), :] = d_window[pl.ds(0, HALO), :]

    keep_halo = (chunk > 0).astype(F32)
    window[pl.ds(0, HALO), :width] = halo_ref[...] * keep_halo
    window[pl.ds(0, HALO), width:] = bc_halo_ref[...] * keep_halo
    window[pl.ds(HALO, CHUNK), :width] = conv_ref[...]
    window[pl.ds(HALO, CHUNK), width:] = bc_ref[...]
    meta = meta_ref[...]
    pre = pre_ref[...]
    sig = sigmoid(pre)
    act = pre * sig
    slope = sig * (1.0 + pre * (1.0 - sig))
    mixer_in = act[:, :width]
    input_mat = act[:, width : width + STATE].astype(BF16)
    output_mat = act[:, width + STATE :].astype(BF16)
    below = triangle(CHUNK)
    lower = below.astype(F32)
    visible = below & (meta[:, 5:6] == seg_row_ref[0])
    step, cumulative = save_ref[:, :LANES], save_ref[:, LANES:]
    cum_rows = cumulative.T
    expand = head_expand(width)
    step_l = lanes_ref[:, :width]
    from_prev_l = lanes_ref[:, width : 2 * width]
    to_end_l = lanes_ref[:, 2 * width :]
    passing = from_prev_l[CHUNK - 1 : CHUNK]
    weighted = mixer_in * step_l
    weighted_b = weighted.astype(BF16)
    scores = mm(output_mat, input_mat, NT)

    gate_rms = jnp.broadcast_to(rms_ref[...], (8, CHUNK)).T[:, 0:1]
    inner_dot = jnp.broadcast_to(dots_ref[...], (8, CHUNK)).T[:, 0:1]
    gate = gate_ref[...]
    gate_sig = sigmoid(gate)
    gate_act = gate * gate_sig
    core = core_ref[...]
    gated = core * gate_act
    d_normed = d_normed_ref[...]
    d_gated = gate_rms * params_ref[8:9, :width] * d_normed - gated * (
        (gate_rms * gate_rms * gate_rms) * inner_dot / inner
    )
    ggain_ref[0:1] += jnp.sum(d_normed * gated * gate_rms, 0, keepdims=True)
    d_core = d_gated * gate_act
    dz_ref[:, :width] = (d_gated * core * (gate_sig * (1.0 + gate * (1.0 - gate_sig)))).astype(BF16)

    d_core_b = d_core.astype(BF16)
    d_core_r = d_core_b.astype(F32)
    incoming_b = states_ref[0]
    d_outgoing = d_state[...]
    d_outgoing_b = d_outgoing.astype(BF16)
    ended = (weighted * to_end_l).astype(BF16)
    after = mm(input_mat, d_outgoing_b) * to_end_l
    scaled_d = (d_core * from_prev_l).astype(BF16)
    d_output = mm(scaled_d, incoming_b, NT)
    d_input = mm(ended, d_outgoing_b, NT)
    d_scores = jnp.zeros((CHUNK, CHUNK), F32)
    d_weighted_parts = []
    for pair in range(width // LANES):
        lanes = slice(pair * LANES, (pair + 1) * LANES)
        first, second = split_pair(weighted_b[:, lanes])
        d_first, d_second = split_pair(d_core_b[:, lanes])
        both_d = mm(d_core_b[:, lanes], jnp.concatenate([first, second], 0), NT)
        mixed = []
        for side, head in enumerate((2 * pair, 2 * pair + 1)):
            gap = cumulative[:, head : head + 1] - cum_rows[head : head + 1, :]
            decay = jnp.exp(jnp.where(visible, gap, NEGATIVE))
            mixed.append((decay * scores).astype(BF16))
            d_scores = d_scores + both_d[:, side * CHUNK : (side + 1) * CHUNK] * decay
        d_weighted_parts.append(
            mm(jnp.concatenate(mixed, 0), jnp.concatenate([d_first, d_second], 0), TN)
        )
    d_within = jnp.concatenate(d_weighted_parts, 1)
    d_scores_b = d_scores.astype(BF16)
    d_output = d_output + mm(d_scores_b, input_mat)
    d_input = d_input + mm(d_scores_b, output_mat, TN)
    d_weighted = d_within + after

    reached = core - params_ref[7:8, :width] * mixer_in
    near = gather_heads(d_core_r * reached - weighted_b.astype(F32) * d_within, expand)
    far_in = gather_heads(weighted * after, expand)
    carried = jnp.sum(d_outgoing * incoming_b.astype(F32), 0, keepdims=True) * passing
    flow = gather_heads(jnp.broadcast_to(carried, (8, width)), expand)[0:1]
    d_rate = mm_exact(lower, near, TN) + (mm_exact(lower, far_in) - far_in) + flow
    d_step = gather_heads(mixer_in * d_weighted, expand) + d_rate * params_ref[6:7, :LANES]
    slope_dt = sigmoid(dt_ref[...] + params_ref[5:6, :LANES])
    d_dt = d_step * slope_dt
    head_lane = lax.broadcasted_iota(jnp.int32, d_dt.shape, 1) < width // HEAD_DIM
    d_dt = jnp.where(head_lane, d_dt, 0.0)
    dz_ref[:, 2 * width :] = d_dt.astype(BF16)
    ghead_ref[0:1, :LANES] += jnp.sum(d_dt, 0, keepdims=True)
    ghead_ref[0:1, LANES:] += jnp.sum(d_rate * (step * params_ref[6:7, :LANES]), 0, keepdims=True)
    gskip_ref[0:1] += jnp.sum(d_core * mixer_in, 0, keepdims=True)
    d_state[...] = passing * d_outgoing + mm(output_mat, scaled_d, TN)

    d_mixer = d_weighted * step_l + d_core * params_ref[7:8, :width]
    d_pre_x = d_mixer * slope[:, :width]
    d_pre_b = d_input * slope[:, width : width + STATE]
    d_pre_c = d_output * slope[:, width + STATE :]
    d_window[pl.ds(0, CHUNK), :width] = d_pre_x
    d_window[pl.ds(0, CHUNK), width : width + STATE] = d_pre_b
    d_window[pl.ds(0, CHUNK), width + STATE :] = d_pre_c
    d_pre = d_window[pl.ds(0, CHUNK), :]
    gconv_ref[4:5] += jnp.sum(d_pre, 0, keepdims=True)
    gconv_ref[0:1] += jnp.sum(d_pre * window[pl.ds(HALO, CHUNK), :], 0, keepdims=True)
    total = params_ref[0:1] * d_pre
    for back in (1, 2, 3):
        gconv_ref[back : back + 1] += jnp.sum(
            d_pre * (window[pl.ds(HALO - back, CHUNK), :] * meta[:, back : back + 1]), 0, keepdims=True
        )
        total = total + params_ref[back : back + 1] * (
            d_window[pl.ds(back, CHUNK), :] * meta_next_ref[:, back : back + 1]
        )
    dz_ref[:, width : 2 * width] = total[:, :width].astype(BF16)
    dbc_ref[...] = total[:, width:].astype(BF16)


def ssm_backward(
    inner, projected, bc_pre, meta, meta_next, seg_row, params, core, d_normed, rms, dots, states,
    pre, lanes, save,
):
    length, width = core.shape
    chunks = length // CHUNK
    back = lambda c: chunks - 1 - c
    row = lambda n, at=0: pl.BlockSpec((CHUNK, n), lambda c: (back(c), at))
    fixed = lambda a: pl.BlockSpec(a.shape, lambda c: (0,) * a.ndim)
    ahead = lambda n, at=0: pl.BlockSpec(
        (HALO, n), lambda c: (jnp.maximum(back(c) * (CHUNK // HALO) - 1, 0), at)
    )
    whole = lambda *s: pl.BlockSpec(s, lambda c: (0, 0))
    channels = width + 2 * STATE
    return pl.pallas_call(
        functools.partial(backward_kernel, inner),
        grid=(chunks,),
        in_specs=[
            row(width), row(width, 1), ahead(width, 1), row(2 * STATE), ahead(2 * STATE),
            row(LANES, 2 * width // LANES), row(8), row(8),
            pl.BlockSpec((1, 1, CHUNK), lambda c: (back(c), 0, 0)),
            fixed(params),
            row(width), row(width),
            pl.BlockSpec((1, CHUNK), lambda c: (0, back(c))), pl.BlockSpec((1, CHUNK), lambda c: (0, back(c))),
            pl.BlockSpec((1, STATE, width), lambda c: (back(c), 0, 0)),
            row(channels), row(3 * width), row(2 * LANES),
        ],
        out_specs=[
            row(2 * width + LANES), row(2 * STATE),
            whole(8, channels), whole(8, 2 * LANES), whole(8, width), whole(8, width),
        ],
        out_shape=[
            jax.ShapeDtypeStruct((length, 2 * width + LANES), BF16),
            jax.ShapeDtypeStruct((length, 2 * STATE), BF16),
            jax.ShapeDtypeStruct((8, channels), F32),
            jax.ShapeDtypeStruct((8, 2 * LANES), F32),
            jax.ShapeDtypeStruct((8, width), F32),
            jax.ShapeDtypeStruct((8, width), F32),
        ],
        scratch_shapes=[
            pltpu.VMEM((CHUNK + HALO, channels), F32),
            pltpu.VMEM((CHUNK + HALO, channels), F32),
            pltpu.VMEM((STATE, width), F32),
        ],
        name="ssm_backward",
    )(projected, projected, projected, bc_pre, bc_pre, projected, meta, meta_next, seg_row, params,
      core, d_normed, rms, dots, states, pre, lanes, save)


def token_meta(segment):
    length = segment.shape[0]
    chunks = length // CHUNK
    by_chunk = segment.reshape(chunks, CHUNK)
    final = by_chunk[:, -1:]
    ahead = jnp.concatenate([jnp.full((1, 1), -1, jnp.int32), final[:-1]], 0)
    from_prev = (by_chunk == ahead).reshape(length)
    keep_end = (by_chunk == final).reshape(length)
    padded = jnp.concatenate([jnp.full((3,), -1, jnp.int32), segment, jnp.full((3,), -1, jnp.int32)])
    behind = [padded[3 - k : 3 - k + length] == segment for k in (1, 2, 3)]
    after = [padded[3 + k : 3 + k + length] == segment for k in (1, 2, 3)]
    none = jnp.zeros((length,), F32)
    stack = lambda columns: jnp.stack([c.astype(F32) for c in columns], 1)
    meta = stack([from_prev] + behind + [keep_end, segment, none, none])
    meta_next = stack([none] + after + [none] * 4)
    return meta, meta_next, segment.astype(F32).reshape(chunks, 1, CHUNK)


MESH = pl.DeviceIdType.MESH
EPSILON = 1e-05
MIB = 1 << 20


def remote(source, target, send_sem, recv_sem, where):
    return pltpu.make_async_remote_copy(
        src_ref=source, dst_ref=target, send_sem=send_sem, recv_sem=recv_sem, device_id=where, device_id_type=MESH
    )


def rows_at(index, count):
    return pl.ds(pl.multiple_of(index * count, 16), count)


def greet(tensor_size, dp_size):
    line, plane = lax.axis_index("tensor"), lax.axis_index("dp")
    barrier = pltpu.get_barrier_semaphore()
    for step in range(1, tensor_size):
        pl.semaphore_signal(
            barrier, inc=1, device_id={"tensor": lax.rem(line + step, tensor_size)}, device_id_type=MESH
        )
    for step in range(1, dp_size):
        pl.semaphore_signal(barrier, inc=1, device_id={"dp": lax.rem(plane + step, dp_size)}, device_id_type=MESH)
    pl.semaphore_wait(barrier, tensor_size - 1 + dp_size - 1)


def flip(index, offset):
    bit = 1
    while bit <= offset:
        if offset & bit:
            index = index + bit - 2 * bit * lax.rem(index // bit, 2)
        bit *= 2
    return index


def entry_kernel(
    tensor_size, dp_size,
    tok_ref, wa_ref, wo_ref, wb_ref, gain_ref, tok_all, wa_all, wo_all, wb_all, gain_all,
    own_sem, right_send, right_recv, left_send, left_recv,
    plane_send, plane_recv, half_send, half_recv, pass_send, pass_recv, small_send, small_recv,
):
    line, plane = lax.axis_index("tensor"), lax.axis_index("dp")
    core, chip, chips = lax.rem(plane, 2), plane // 2, dp_size // 2
    relay = chips == 4
    direct = (1, 2) if relay else tuple(range(1, chips))
    sibling = {"dp": plane + 1 - 2 * core}
    count = tok_ref.shape[0] // PIECES
    smalls = ((wb_ref, wb_all), (gain_ref, gain_all))
    greet(tensor_size, dp_size)

    def small_out(which, offset):
        source, place = smalls[which]
        return remote(
            source, place.at[plane, line], small_send.at[which, offset], small_recv.at[which, offset],
            {"tensor": lax.rem(line + offset, tensor_size)},
        )

    for which in (0, 1):
        for offset in range(1, tensor_size):
            small_out(which, offset).start()
    own = [
        pltpu.make_async_copy(wb_ref, wb_all.at[plane, line], own_sem.at[0]),
        pltpu.make_async_copy(gain_ref, gain_all.at[plane, line], own_sem.at[1]),
        pltpu.make_async_copy(tok_ref, tok_all.at[rows_at(line, tok_ref.shape[0])], own_sem.at[2]),
        pltpu.make_async_copy(wa_ref, wa_all.at[rows_at(plane, wa_ref.shape[0])], own_sem.at[3]),
        pltpu.make_async_copy(wo_ref, wo_all.at[rows_at(plane, wo_ref.shape[0])], own_sem.at[4]),
    ]

    def token_copy(step, piece, to_right, arriving=False):
        origin = line - step if to_right else line + step
        if arriving:
            origin = origin - 1 if to_right else origin + 1
        origin = jnp.clip(origin, 0, tensor_size - 1)
        place = tok_all.at[rows_at(origin * PIECES + piece, count)]
        source = tok_ref.at[pl.ds(piece * count, count)] if step == 0 and not arriving else place
        neighbour = line + 1 if to_right != arriving else line - 1
        return remote(
            source, place,
            (right_send if to_right else left_send).at[step, piece],
            (right_recv if to_right else left_recv).at[step, piece],
            {"tensor": jnp.clip(neighbour, 0, tensor_size - 1)},
        )

    def sends(step, to_right):
        if to_right:
            return (line - step >= 0) & (line + 1 < tensor_size)
        return (line + step < tensor_size) & (line >= 1)

    def forward_tokens(step):
        for piece in range(PIECES):
            for to_right in (True, False):
                @pl.when(sends(step, to_right))
                def _():
                    if step > 0:
                        token_copy(step - 1, piece, to_right, True).wait_recv()
                    token_copy(step, piece, to_right).start()

    def shard(ref, source):
        rows = source.shape[0]
        return lambda d, half=None: ref.at[
            rows_at(d, rows) if half is None else pl.ds(pl.multiple_of(d * rows + half * (rows // 2), 16), rows // 2)
        ]

    def block(ref):
        n = ref.shape[1] // 2
        return lambda d, half=None: ref.at[d] if half is None else ref.at[d, pl.ds(half * n, n)]

    stacks = [
        (wo_ref, shard(wo_all, wo_ref)),
        (None, block(wb_all)),
        (None, block(gain_all)),
        (wa_ref, shard(wa_all, wa_ref)),
    ]

    def device(offset, side):
        return 2 * flip(chip, offset) + side

    def plane_copy(which, offset):
        source, place = stacks[which]
        return remote(
            place(plane) if source is None else source, place(plane),
            plane_send.at[which, offset], plane_recv.at[which, offset], {"dp": device(offset, core)},
        )

    def plane_arrival(which, offset):
        origin = device(offset, core)
        place = stacks[which][1](origin)
        return remote(place, place, plane_send.at[which, offset], plane_recv.at[which, offset], {"dp": origin})

    def half_copy(which, half):
        place = stacks[which][1](device(half + 1, core), half)
        return remote(
            place, place, half_send.at[which, half], half_recv.at[which, half], {"dp": device(2 - half, core)}
        )

    def half_arrival(which, half):
        place = stacks[which][1](device(3, core), half)
        return remote(
            place, place, half_send.at[which, half], half_recv.at[which, half], {"dp": device(2 - half, core)}
        )

    def pass_copy(which, offset, arriving=False):
        source, place = stacks[which]
        origin = device(offset, 1 - core if arriving else core)
        return remote(
            source if offset == 0 and source is not None and not arriving else place(origin), place(origin),
            pass_send.at[which, offset], pass_recv.at[which, offset], sibling,
        )

    def plane_start(which):
        for offset in direct:
            plane_copy(which, offset).start()

    def plane_next(which):
        for offset in direct:
            plane_arrival(which, offset).wait_recv()
            if relay:
                half_copy(which, offset - 1).start()
            pass_copy(which, offset).start()

    def plane_last(which):
        if relay:
            half_arrival(which, 0).wait_recv()
            half_arrival(which, 1).wait_recv()
            pass_copy(which, 3).start()

    forward_tokens(0)
    plane_start(0)
    for copy in own:
        copy.start()
    own[0].wait()
    own[1].wait()
    for which in (0, 1):
        for offset in range(1, tensor_size):
            small_out(which, offset).wait_recv()
    plane_start(1)
    plane_start(2)
    plane_start(3)
    for which in range(4):
        pass_copy(which, 0).start()
    plane_next(0)
    plane_next(1)
    plane_next(2)
    forward_tokens(1)
    plane_next(3)
    for which in range(3):
        plane_last(which)
    for step in range(2, tensor_size - 1):
        forward_tokens(step)
    plane_last(3)

    for to_right in (True, False):
        for step in range(tensor_size - 1):
            arrives = line - 1 - step >= 0 if to_right else line + 1 + step < tensor_size
            at_end = line + 1 == tensor_size if to_right else line == 0

            @pl.when(arrives & at_end)
            def _():
                for piece in range(PIECES):
                    token_copy(step, piece, to_right, True).wait_recv()

            @pl.when(sends(step, to_right))
            def _():
                for piece in range(PIECES):
                    token_copy(step, piece, to_right).wait_send()

    for which in range(4):
        for offset in range(chips):
            pass_copy(which, offset, True).wait_recv()
            pass_copy(which, offset).wait_send()
        for offset in direct:
            plane_copy(which, offset).wait_send()
        if relay:
            half_copy(which, 0).wait_send()
            half_copy(which, 1).wait_send()
    for which in (0, 1):
        for offset in range(1, tensor_size):
            small_out(which, offset).wait_send()
    for copy in own[2:]:
        copy.wait()


PIECES = 2


def entry(tensor_size, dp_size, tokens, wa, wo, wb, gain):
    vmem = pl.BlockSpec(memory_space=pltpu.VMEM)
    anywhere = pl.BlockSpec(memory_space=pl.ANY)
    dma = pltpu.SemaphoreType.DMA
    chips = dp_size // 2
    return pl.pallas_call(
        functools.partial(entry_kernel, tensor_size, dp_size),
        in_specs=[vmem] * 5,
        out_specs=[anywhere] * 5,
        out_shape=[
            jax.ShapeDtypeStruct((tensor_size * tokens.shape[0], tokens.shape[1]), BF16),
            jax.ShapeDtypeStruct((dp_size * wa.shape[0], wa.shape[1]), BF16),
            jax.ShapeDtypeStruct((dp_size * wo.shape[0], wo.shape[1]), BF16),
            jax.ShapeDtypeStruct((dp_size, tensor_size) + wb.shape, BF16),
            jax.ShapeDtypeStruct((dp_size, tensor_size) + gain.shape, BF16),
        ],
        scratch_shapes=[
            dma((5,)), *[dma((tensor_size, PIECES))] * 4,
            dma((4, chips)), dma((4, chips)), dma((4, 2)), dma((4, 2)), dma((4, chips)), dma((4, chips)),
            dma((2, tensor_size)), dma((2, tensor_size)),
        ],
        compiler_params=pltpu.CompilerParams(collective_id=0, has_side_effects=True),
        name="entry_gather",
    )(tokens, wa, wo, wb, gain)


def stat_kernel(tensor_size, inner, own_ref, out_ref, slots, send_sem, recv_sem):
    line = lax.axis_index("tensor")
    barrier = pltpu.get_barrier_semaphore()
    for offset in range(1, tensor_size):
        pl.semaphore_signal(
            barrier, inc=1, device_id={"tensor": lax.rem(line + offset, tensor_size)}, device_id_type=MESH
        )
    pl.semaphore_wait(barrier, tensor_size - 1)
    copies = [
        remote(
            own_ref, slots.at[offset], send_sem.at[offset], recv_sem.at[offset],
            {"tensor": lax.rem(line + offset, tensor_size)},
        )
        for offset in range(1, tensor_size)
    ]
    for copy in copies:
        copy.start()
    total = own_ref[...]
    for offset, copy in enumerate(copies, 1):
        copy.wait_recv()
        total = total + slots[offset]
    out_ref[...] = total if inner is None else lax.rsqrt(total / inner + EPSILON)
    for copy in copies:
        copy.wait_send()


def stat_sum(tensor_size, inner, own, identity):
    vmem = pl.BlockSpec(memory_space=pltpu.VMEM)
    dma = pltpu.SemaphoreType.DMA
    return pl.pallas_call(
        functools.partial(stat_kernel, tensor_size, inner),
        in_specs=[vmem],
        out_specs=vmem,
        out_shape=jax.ShapeDtypeStruct(own.shape, F32),
        scratch_shapes=[pltpu.VMEM((tensor_size,) + own.shape, F32), dma((tensor_size,)), dma((tensor_size,))],
        compiler_params=pltpu.CompilerParams(collective_id=identity, has_side_effects=True),
        name="dot_sum" if inner is None else "rms_sum",
    )(own)


BAND = 16


def add_rows(target, terms, count):
    def step(index, carry):
        at = pl.multiple_of(index * BAND, BAND)
        total = terms[0](at)
        for term in terms[1:]:
            total = total + term(at)
        target(at, total)
        return carry

    lax.fori_loop(0, count // BAND, step, 0)


def exit_kernel(
    tensor_size, dp_size,
    ga_ref, go_ref, gb_ref, small_ref,
    sa_ref, so_ref, sb_ref, plane_sum_ref, all_sum_ref,
    near_a, near_o, near_b, far_a, far_o, far_b, mid_b, b_slots, pair_ref, plane_slots, line_slots,
    near_send, near_recv, far_send, far_recv,
    b_send, b_recv, plane_send, plane_recv, line_send, line_recv,
):
    line, plane = lax.axis_index("tensor"), lax.axis_index("dp")
    core, chip, chips = lax.rem(plane, 2), plane // 2, dp_size // 2
    relay = chips == 4
    sibling = {"dp": plane + 1 - 2 * core}
    greet(tensor_size, dp_size)

    grads = [(ga_ref, near_a, far_a), (go_ref, near_o, far_o), (gb_ref, near_b, far_b)]
    order = [3, 1, 2, 0] if relay else list(range(1, chips)) + [0]
    arrays = (2, 0, 1)

    def device(offset, side):
        return 2 * flip(chip, offset) + side

    def near_copy(which, offset):
        grad, near, _ = grads[which]
        return remote(
            grad.at[rows_at(device(offset, 1 - core), near.shape[1])], near.at[offset],
            near_send.at[which, offset], near_recv.at[which, offset], sibling,
        )

    def far_copy(which, offset, half, towards):
        _, near, far = grads[which]
        span = pl.ds(half * (near.shape[1] // 2), near.shape[1] // 2)
        return remote(
            near.at[offset, span], far.at[offset, span],
            far_send.at[which, offset, half], far_recv.at[which, offset, half], {"dp": device(towards, core)},
        )

    def small_plane(offset):
        if offset == 0:
            return remote(small_ref, plane_slots.at[0], plane_send.at[0], plane_recv.at[0], sibling)
        return remote(
            pair_ref, plane_slots.at[offset], plane_send.at[offset], plane_recv.at[offset],
            {"dp": device(offset, core)},
        )

    def small_line(offset):
        return remote(
            plane_sum_ref.at[pl.ds(8, 8)], line_slots.at[offset], line_send.at[offset], line_recv.at[offset],
            {"tensor": lax.rem(line + offset, tensor_size)},
        )

    def near_sum(offset):
        owner = device(offset, core)
        for which in arrays:
            grad, near, _ = grads[which]
            near_copy(which, offset).wait_recv()
            base = owner * near.shape[1]

            def both(at, near=near, grad=grad, base=base):
                mine = grad[pl.ds(pl.multiple_of(base + at, BAND), BAND), :]
                return near[offset, pl.ds(at, BAND), :].astype(F32) + mine.astype(F32)

            def put(at, total, near=near):
                near[offset, pl.ds(at, BAND), :] = total.astype(BF16)

            add_rows(put, [both], near.shape[1])

    def merge(offset, half, source):
        for which in arrays:
            _, near, far = grads[which]
            span = near.shape[1] // 2
            far_copy(which, 3, half, source).wait_recv()

            def both(at, near=near, far=far, span=span):
                at = half * span + at
                return near[offset, pl.ds(at, BAND), :].astype(F32) + far[3, pl.ds(at, BAND), :].astype(F32)

            def put(at, total, near=near, span=span):
                near[offset, pl.ds(half * span + at, BAND), :] = total.astype(BF16)

            add_rows(put, [both], span)
            far_copy(which, offset, half, offset).start()

    for which in arrays:
        near_copy(which, order[0]).start()
    small_plane(0).start()
    for offset in order[1:]:
        for which in arrays:
            near_copy(which, offset).start()

    for offset in order[:-1]:
        near_sum(offset)
        for which in arrays:
            if not relay:
                far_copy(which, offset, 0, offset).start()
                far_copy(which, offset, 1, offset).start()
            elif offset == 3:
                far_copy(which, 3, 0, 1).start()
                far_copy(which, 3, 1, 2).start()
            else:
                far_copy(which, offset, offset - 1, offset).start()
        if offset == order[0]:
            small_plane(0).wait_recv()
            pair_ref[...] = small_ref[...] + plane_slots[0]
            for away in range(1, chips):
                small_plane(away).start()
    near_sum(0)
    if relay:
        merge(1, 1, 2)
        merge(2, 0, 1)
    total = pair_ref[...]
    for offset in range(1, chips):
        small_plane(offset).wait_recv()
        total = total + plane_slots[offset]
    plane_sum_ref[...] = total
    for offset in range(1, tensor_size):
        small_line(offset).start()

    direct = (1, 2) if relay else tuple(range(1, chips))
    block = sb_ref.shape[0]
    for which, out in ((2, mid_b), (0, sa_ref), (1, so_ref)):
        _, near, far = grads[which]
        for offset in direct:
            for half in (0, 1):
                far_copy(which, offset, half, offset).wait_recv()
        terms = [lambda at, near=near: near[0, pl.ds(at, BAND), :].astype(F32)] + [
            lambda at, far=far, offset=offset: far[offset, pl.ds(at, BAND), :].astype(F32) for offset in direct
        ]

        def put(at, total, out=out):
            out[pl.ds(at, BAND), :] = total

        add_rows(put, terms, near.shape[1])
        if which == 2:
            b_copies = [
                remote(
                    mid_b.at[rows_at(lax.rem(line + offset, tensor_size), block)], b_slots.at[offset],
                    b_send.at[offset], b_recv.at[offset], {"tensor": lax.rem(line + offset, tensor_size)},
                )
                for offset in range(1, tensor_size)
            ]
            for copy in b_copies:
                copy.start()

    total = plane_sum_ref[8:]
    for offset in range(1, tensor_size):
        small_line(offset).wait_recv()
        total = total + line_slots[offset]
    all_sum_ref[...] = total

    total = mid_b[rows_at(line, block), :]
    for offset, copy in enumerate(b_copies, 1):
        copy.wait_recv()
        total = total + b_slots[offset]
    sb_ref[...] = total

    for which in range(3):
        for offset in range(chips):
            near_copy(which, offset).wait_send()
            if offset:
                for half in (0, 1):
                    towards = offset if offset != 3 or not relay else half + 1
                    far_copy(which, offset, half, towards).wait_send()
    for copy in b_copies:
        copy.wait_send()
    for offset in range(chips):
        small_plane(offset).wait_send()
    for offset in range(1, tensor_size):
        small_line(offset).wait_send()


def leave(tensor_size, dp_size, ga, go, gb, small):
    vmem = pl.BlockSpec(memory_space=pltpu.VMEM)
    dma = pltpu.SemaphoreType.DMA
    chips = dp_size // 2
    ra, ro, rb = (g.shape[0] // dp_size for g in (ga, go, gb))
    block = rb // tensor_size
    slots = lambda n, r, c, t=BF16: pltpu.VMEM((n, r, c), t)
    return pl.pallas_call(
        functools.partial(exit_kernel, tensor_size, dp_size),
        in_specs=[vmem] * 4,
        out_specs=[vmem] * 5,
        out_shape=[
            jax.ShapeDtypeStruct((ra, ga.shape[1]), F32),
            jax.ShapeDtypeStruct((ro, go.shape[1]), F32),
            jax.ShapeDtypeStruct((block, gb.shape[1]), F32),
            jax.ShapeDtypeStruct(small.shape, F32),
            jax.ShapeDtypeStruct((8, small.shape[1]), F32),
        ],
        scratch_shapes=[
            slots(chips, ra, ga.shape[1]), slots(chips, ro, go.shape[1]), slots(chips, rb, gb.shape[1]),
            slots(chips, ra, ga.shape[1]), slots(chips, ro, go.shape[1]), slots(chips, rb, gb.shape[1]),
            pltpu.VMEM((rb, gb.shape[1]), F32), slots(tensor_size, block, gb.shape[1], F32),
            pltpu.VMEM(small.shape, F32), slots(chips, *small.shape, F32), slots(tensor_size, 8, small.shape[1], F32),
            dma((3, chips)), dma((3, chips)), dma((3, chips, 2)), dma((3, chips, 2)),
            dma((tensor_size,)), dma((tensor_size,)), dma((chips,)), dma((chips,)),
            dma((tensor_size,)), dma((tensor_size,)),
        ],
        compiler_params=pltpu.CompilerParams(collective_id=2, has_side_effects=True, vmem_limit_bytes=60 * MIB),
        name="exit_reduce",
    )(ga, go, gb, small)


STEPS = 4


def finish_kernel(
    width, bc_rows,
    tok_ref, cot_ref, gain_ref, mixed_ref, d_own_ref, sa_ref, dt_ref, sb_ref, plane_ref, all_ref,
    layer_ref, dtok_ref, gzx_ref, gbc_ref, gdt_ref, cxw_ref, cxb_ref, cbw_ref, cbb_ref, dtb_ref, alog_ref, skip_ref,
    gate_ref,
):
    gain = gain_ref[...]

    def step(index, carry):
        at = pl.ds(pl.multiple_of(index * BAND, BAND), BAND)
        tokens = tok_ref[at, :].astype(F32)
        layer_ref[at, :] = (tokens + mixed_ref[at, :].astype(F32)).astype(BF16)
        inv = lax.rsqrt(jnp.mean(tokens * tokens, -1, keepdims=True) + EPSILON)
        d_own = d_own_ref[at, :].astype(F32)
        slope = gain * d_own
        dtok_ref[at, :] = cot_ref[at, :].astype(F32) + (
            inv * slope - tokens * (inv * inv * inv) * jnp.mean(tokens * slope, -1, keepdims=True)
        )
        return carry

    lax.fori_loop(0, tok_ref.shape[0] // BAND, step, 0)
    gzx_ref[:, 0, :] = sa_ref[:, :width]
    gzx_ref[:, 1, :] = sa_ref[:, width : 2 * width]

    @pl.when(pl.program_id(0) == 0)
    def _():
        gbc_ref[...] = sb_ref[:bc_rows]
        heads = dtb_ref.shape[1]
        gdt_ref[...] = dt_ref[...].T[:heads]
        cxw_ref[...] = plane_ref[:4, :width]
        cxb_ref[...] = plane_ref[4:5, :width]
        gate_ref[...] = plane_ref[5:6, :width]
        dtb_ref[...] = plane_ref[6:7, :heads]
        alog_ref[...] = plane_ref[6:7, LANES : LANES + heads]
        cbw_ref[...] = all_ref[1:5, : 2 * STATE]
        cbb_ref[...] = all_ref[5:6, : 2 * STATE]
        per_head = gather_heads(jnp.broadcast_to(plane_ref[7:8, :width], (8, width)), head_expand(width))
        skip_ref[...] = per_head[0:1, :heads]


def finish(width, bc_rows, heads, tokens, cotangent, gain, mixed, d_own, sa, sb, plane_sum, all_sum):
    row = lambda a: pl.BlockSpec((a[0] // STEPS,) + a[1:], lambda i: (i,) + (0,) * (len(a) - 1))
    last = lambda a: pl.BlockSpec((a[0], LANES), lambda i: (0, 2 * width // LANES))
    fixed = lambda a: pl.BlockSpec(a, lambda i: (0, 0))
    shapes = [
        (tokens.shape, BF16), (tokens.shape, F32), ((sa.shape[0], 2, width), F32), ((bc_rows, sb.shape[1]), F32),
        ((heads, sa.shape[0]), F32), ((4, width), F32), ((1, width), F32), ((4, 2 * STATE), F32), ((1, 2 * STATE), F32),
        ((1, heads), F32), ((1, heads), F32), ((1, heads), F32), ((1, width), F32),
    ]
    kinds = [row, row, row] + [fixed] * 10
    args = (tokens, cotangent, gain, mixed, d_own, sa, sa, sb, plane_sum, all_sum)
    inputs = [row, row, fixed, row, row, row, last, fixed, fixed, fixed]
    return pl.pallas_call(
        functools.partial(finish_kernel, width, bc_rows),
        grid=(STEPS,),
        in_specs=[kind(a.shape) for kind, a in zip(inputs, args)],
        out_specs=[kind(s[0]) for kind, s in zip(kinds, shapes)],
        out_shape=[jax.ShapeDtypeStruct(*s) for s in shapes],
        compiler_params=pltpu.CompilerParams(vmem_limit_bytes=61 * MIB),
        name="finish",
    )(*args)


def pad_lanes(values, size):
    return jnp.pad(values, [(0, 0)] * (values.ndim - 1) + [(0, size - values.shape[-1])])


def dot(a, b, dims, out=F32):
    return lax.dot_general(a, b, (dims, ((), ())), preferred_element_type=out)


def body(
    tensor_size, dp_size,
    tokens, segment_ids, cotangent, norm_gain, w_zx, w_bc, w_dt, conv_x_w, conv_x_b, conv_bc_w, conv_bc_b,
    dt_bias, a_log, d_skip, gate_gain, w_out,
):
    own_rows, model = tokens.shape
    weight_rows, _, width = w_zx.shape
    heads_here = w_dt.shape[1]
    inner = width * tensor_size
    bc_rows = w_bc.shape[0]
    bc_padded = -(-bc_rows // 16) * 16
    assert segment_ids.shape[0] == 1

    wa = jnp.concatenate([w_zx.reshape(weight_rows, 2 * width), pad_lanes(w_dt, LANES)], 1)
    wo = w_out.T
    wb = jnp.pad(w_bc, ((0, bc_padded - bc_rows), (0, 0)))
    gain_block = jnp.broadcast_to(pad_lanes(norm_gain[None], LANES), (16, LANES))
    tok_all, wa_all, wo_all, wb_all, gain_all = entry(tensor_size, dp_size, tokens, wa, wo, wb, gain_block)
    cot_late, _ = lax.optimization_barrier((cotangent, gain_all))
    d_out = lax.all_gather(cot_late, "tensor", axis=0, tiled=True)

    gain = gain_all[:, :, 0, : norm_gain.shape[0]].reshape(1, model).astype(F32)
    wb_all = wb_all[:, :, :bc_rows].reshape(model, 2 * STATE)
    meta, meta_next, seg_row = token_meta(segment_ids[0])
    channels = width + 2 * STATE
    params = jnp.concatenate(
        [
            jnp.concatenate([conv_x_w, conv_bc_w], 1),
            jnp.concatenate([conv_x_b, conv_bc_b])[None],
            pad_lanes(dt_bias[None], channels),
            pad_lanes(-jnp.exp(a_log)[None], channels),
            pad_lanes(jnp.repeat(d_skip, HEAD_DIM)[None], channels),
            pad_lanes(gate_gain[None], channels),
            jnp.zeros((7, channels), F32),
        ],
        0,
    )

    x_all = tok_all.astype(F32)
    inv_all = lax.rsqrt(jnp.mean(x_all * x_all, -1, keepdims=True) + EPSILON)
    normed_in = (x_all * inv_all * gain).astype(BF16)
    projected = dot(normed_in, wa_all, ((1,), (0,)))
    bc_pre = dot(normed_in, wb_all, ((1,), (0,)))
    core, gated, states, sums, pre, lanes, small_save = ssm_forward(projected, bc_pre, meta, seg_row, params)

    gate_row = gate_gain[None]
    rms = stat_sum(tensor_size, inner, sums[:1], 1)
    normed_out = (gated * rms[0][:, None] * gate_row).astype(BF16)
    mixed = dot(normed_out, wo_all, ((1,), (1,)), BF16)
    mixed_own = lax.psum_scatter(mixed, "tensor", scatter_dimension=0, tiled=True)
    d_out, mixed = lax.optimization_barrier((d_out, mixed))
    d_normed = dot(d_out, wo_all, ((1,), (0,)))
    inner_part = jnp.sum(gated * gate_row * d_normed, -1)[None]
    dots = stat_sum(tensor_size, None, inner_part, 3)

    dz, dbc, gconv, ghead, ggain, gskip = ssm_backward(
        inner, projected, bc_pre, meta, meta_next, seg_row, params, core, d_normed, rms, dots, states, pre, lanes, small_save
    )
    go = dot(d_out, normed_out, ((0,), (0,)), BF16)
    part = (dot(dz, wa_all, ((1,), (1,))) + dot(dbc, wb_all, ((1,), (1,)))).astype(BF16)
    ga = dot(normed_in, dz, ((0,), (0,)), BF16)
    gb = dot(normed_in, dbc, ((0,), (0,)), BF16)
    gb = jnp.pad(
        gb.reshape(dp_size * tensor_size, bc_rows, 2 * STATE), ((0, 0), (0, bc_padded - bc_rows), (0, 0))
    ).reshape(dp_size * tensor_size * bc_padded, 2 * STATE)
    gnorm = jnp.sum(part.astype(F32) * x_all * inv_all, 0)[None]
    packed = jnp.concatenate(
        [
            pad_lanes(gconv[:5, :width], model), pad_lanes(ggain[:1], model), pad_lanes(ghead[:1], model),
            pad_lanes(gskip[:1], model), gnorm, pad_lanes(gconv[:5, width:], model), jnp.zeros((2, model), F32),
        ],
        0,
    )
    d_own = lax.psum_scatter(part, "tensor", scatter_dimension=0, tiled=True)
    ga, part = lax.optimization_barrier((ga, part))
    sa, so, sb, plane_sum, all_sum = leave(tensor_size, dp_size, ga, go, gb, packed)
    layer_out, grad_tokens, gzx, gbc, gdt, cxw, cxb, cbw, cbb, dtb, alog, gsk, ggate = finish(
        width, bc_rows, heads_here, tokens, cotangent, gain, mixed_own, d_own, sa, sb, plane_sum, all_sum
    )
    place = lax.axis_index("dp") * tensor_size + lax.axis_index("tensor")
    own_gain = norm_gain.shape[0]
    return (
        layer_out,
        grad_tokens,
        lax.dynamic_slice(all_sum[0], (place * own_gain,), (own_gain,)),
        gzx, gbc, gdt.T, cxw, cxb[0], cbw, cbb[0], dtb[0], alog[0], gsk[0], ggate[0], so.T,
    )


def solution(mesh):
    in_specs = (
        P(("dp", "tensor"), None),
        P("dp", None),
        P(("dp", "tensor"), None),
        P(("dp", "tensor")),
        P("dp", None, "tensor"),
        P(("dp", "tensor"), None),
        P("dp", "tensor"),
        P(None, "tensor"),
        P("tensor"),
        P(),
        P(),
        P("tensor"),
        P("tensor"),
        P("tensor"),
        P("tensor"),
        P("tensor", "dp"),
    )
    out_specs = (
        P(("dp", "tensor"), None),
        P(("dp", "tensor"), None),
        P(("dp", "tensor")),
        P("dp", None, "tensor"),
        P(("dp", "tensor"), None),
        P("dp", "tensor"),
        P(None, "tensor"),
        P("tensor"),
        P(),
        P(),
        P("tensor"),
        P("tensor"),
        P("tensor"),
        P("tensor"),
        P("tensor", "dp"),
    )
    return jax.shard_map(
        functools.partial(body, mesh.shape["tensor"], mesh.shape["dp"]),
        mesh=mesh, in_specs=in_specs, out_specs=out_specs, check_vma=False,
    )
```

time: 855 us -> 283 us (0.33)
  waiting for transfers between devices: 262 us -> 11.9 us
  blocking collectives: 223 us -> 0 us
  Pallas kernels: 0 us -> 177 us
  matrix products: 150 us -> 55 us
  local copies, waits for them, and re-layouts: 103 us -> 15.2 us
  other arithmetic: 93.6 us -> 8.99 us
    reduce_scatter x5 -> x2, waiting for transfers between devices: 253 us -> 2.21 us  [the longest x1 2.21 us: body(): d_own = lax.psum_scatter(part, 'tensor', scatter_dimension=0, tiled=True)]
    pallas_call x0 -> x7, Pallas kernels: none -> 177 us  [the longest x1 61.7 us: entry(): pl.pallas_call(functools.partial(entry_kernel, tensor_size, dp_size), in_...]
    all_gather x2 -> x0, blocking collectives: 93.6 us -> none  [the longest x1 83.5 us: body(): lax.all_gather(w_bc, ('dp', 'tensor'), axis=0, tiled=True)]
    dot_general x23 -> x9, matrix products: 147 us -> 55 us  [dot(): return lax.dot_general(a, b, (dims, ((), ())), preferred_element_type=out)]
    unnamed x2 -> x0, blocking collectives: 86.7 us -> none
    psum x3 -> x0, blocking collectives: 43.1 us -> none  [the longest x1 23.2 us: body(): lax.psum((g_cxw, g_cxb, g_dtb, g_alog, g_skip, g_gate_gain, g_cbw, g_cbb)...]
    reduce_sum x14 -> x1, other arithmetic: 38.3 us -> 2.99 us  [body(): inv_all = lax.rsqrt(jnp.mean(x_all * x_all, -1, keepdims=True) + EPSILON)]
    reshape x12 -> x0, local copies, waits for them, and re-layouts: 34.5 us -> none  [the longest x4 19.5 us: mixer_sequence(): jax.nn.silu(causal_conv(conv_in, conv_x_w, conv_x_b, segment))]
  transfers between devices with their start and end apart: 11 -> 3, of which waited for: 7 -> 2; matrix products, arithmetic and copies ran while one was open for 24% -> 25% of each run, Pallas kernels for 0% -> 39%
where the time goes in v1:
time: 283 us
  Pallas kernels  177 us (63%)
  matrix products  55 us (19%)
  local copies, waits for them, and re-layouts  15.2 us (5%)
  between operations  14.2 us (5%)
  waiting for transfers between devices  11.9 us (4%)
  other arithmetic  8.99 us (3%)
    pallas_call x1, Pallas kernels, entry(): pl.pallas_call(functools.partial(entry_kernel, tensor_size, dp_size), in_...  61.7 us
    dot_general x9, matrix products, dot(): return lax.dot_general(a, b, (dims, ((), ())), preferred_element_type=out)  55 us
    pallas_call x1, Pallas kernels, leave(): pl.pallas_call(functools.partial(exit_kernel, tensor_size, dp_size), in_s...  49.9 us
    pallas_call x1, Pallas kernels, ssm_backward(): pl.pallas_call(functools.partial(backward_kernel, inner), grid=(chunks,),...  26.6 us
    pallas_call x1, Pallas kernels, ssm_forward(): pl.pallas_call(forward_kernel, grid=(chunks,), in_specs=[row(width), row(...  18.6 us
    pallas_call x2, Pallas kernels, stat_sum(): pl.pallas_call(functools.partial(stat_kernel, tensor_size, inner), in_spe...  14 us
    all_gather x1, waiting for transfers between devices, body(): d_out = lax.all_gather(cot_late, 'tensor', axis=0, tiled=True)  9.63 us
    pallas_call x1, Pallas kernels, finish(): pl.pallas_call(functools.partial(finish_kernel, width, bc_rows), grid=(ST...  6.43 us
  transfers between devices with their start and end apart: 3, of which 2 were waited for; matrix products, arithmetic and copies ran while one was open for 25% of the time, Pallas kernels for 39%

profile of v1, /device:TPU:0, one launch (start us, length us, event | category | flops | bytes accessed | tf_op | source)
XLA Modules:
  0.0 282.5 jit_solution(16380729521140398147)
XLA Ops:
  7.3 0.0 all-gather.2.cloned.1.call-start
  7.3 0.7 pad_bitcast_fusion
  8.0 0.8 copy.52
  8.8 1.1 copy.63
  9.9 0.9 fusion.6.wa_ref
  10.8 0.6 broadcast_in_dim.39.gain_ref
  11.4 61.7 %entry_gather.1 = (bf16[1024,1536]{1,0:T(8,128)(2,1)}, bf16[1536,1664]{1,0:T(8,128)(2,1)}, bf16[1536,768]{1,0:T(8,128)(2,1)}, bf16[8,4,48,256]{3,2,1,0:T(8,128)(2,1)}, bf16[8,4,16,128]{3,2,1,0:T(8,128)(2,1)}) custom-call(bf16[256,1536]{1,0:T(8,128)(2,1)} %tok_ref.3, bf16[192,1664]{1,0:T(8,128)(2,1)} %fusion.6.wa_ref, bf16[192,768]{1,0:T(8,128)(2,1)} %bitcast.58, ...), custom_call_target="tpu_custom_call" | custom-call | tf_op jit(solution)/shard_map/entry_gather/pallas_call | solution.py:628
  73.1 0.0 all-gather.2.cloned.1.call-update
  73.1 0.0 reduce-scatter.3.cloned.1.call-start
  73.2 0.1 slice.56
  73.2 0.1 slice.60
  73.3 0.0 copy-done.9
  73.4 0.1 copy.61
  73.5 0.1 copy.62
  73.6 0.1 broadcast_in_dim.42
  73.6 0.1 broadcast_in_dim_reshape.3
  73.7 0.1 add_bitcast_fusion
  73.8 0.6 convert_bitcast_fusion
  74.4 0.1 eq.59
  74.5 0.1 eq.66
  74.6 0.1 fusion.13
  74.6 0.1 stack.58
  74.7 1.0 copy.55.meta_ref
  75.7 0.8 slice_convert_fusion
  76.6 0.1 reshape.138
  76.6 0.0 copy-done.10
  76.7 1.3 concatenate.34.params_ref
  78.0 3.0 %fusion = f32[1024]{0:T(1024)S(1)} fusion(bf16[1024,1536]{1,0:T(8,128)(2,1)} %get-tuple-element.55), kind=kLoop, calls=%fused_computation.3 | loop fusion | flops 4717568 | bytes 3149824 | tf_op jit(solution)/shard_map/reduce_sum | solution.py:1019
  81.0 0.0 slice-start.1
  81.0 2.0 fusion.26.bc_ref.bc_halo_ref
  83.0 0.0 slice-done.1
  83.0 8.0 %fusion.28.gate_ref.conv_ref.dt_ref.halo_ref = f32[1024,1664]{1,0:T(8,128)} fusion(bf16[1536,1664]{1,0:T(8,128)(2,1)S(1)} %bitcast.78, bf16[1024,1536]{1,0:T(8,128)(2,1)S(1)} %copy-done, f32[1536]{0:T(1024)S(1)} %reshape.138, f32[1024]{0:T(1024)S(1)} %add_rsqrt_fusion), kind=kOutput, calls=%fused_computation.50 | convolution fusion | flops 5240782848 | bytes 15083520 | tf_op jit(solution)/shard_map/dot_general | solution.py:977
  91.0 18.6 %ssm_forward.1 = (f32[1024,768]{1,0:T(8,128)}, f32[1024,768]{1,0:T(8,128)}, bf16[8,128,768]{2,1,0:T(8,128)(2,1)}, f32[8,1024]{1,0:T(8,128)}, f32[1024,1024]{1,0:...) custom-call(f32[1024,1664]{1,0:T(8,128)} %fusion.28.gate_ref.conv_ref.dt_ref.halo_ref, ...), custom_call_target="tpu_custom_call" | custom-call | tf_op jit(solution)/shard_map/ssm_forward/pallas_call | solution.py:162
  109.7 1.4 slice.61.own_ref
  111.0 7.0 %rms_sum.1.rms_ref = f32[1,1024]{1,0:T(1,128)} custom-call(f32[1,1024]{1,0:T(1,128)} %slice.61.own_ref), custom_call_target="tpu_custom_call" | custom-call | tf_op jit(solution)/shard_map/rms_sum/pallas_call | solution.py:678
  118.0 6.9 %fusion.21 = bf16[1024,1536]{1,0:T(8,128)(2,1)} fusion(bf16[1536,768]{1,0:T(8,128)(2,1)} %get-tuple-element.60, f32[1024,768]{1,0:T(8,128)} %get-tuple-element.58, f32[768]{0:T(1024)S(1)} %copy-done.9, f32[1024]{0:T(1024)} %bitcast.63), kind=kOutput, calls=%fused_computation.46 | convolution fusion | flops 2418278400 | bytes 8657920 | tf_op jit(solution)/shard_map/dot_general | solution.py:977
  125.0 0.0 reduce-scatter.3.cloned.1.call-update
  125.0 0.0 reduce-scatter.5.cloned.1.call-start
  125.1 1.0 copy.58.meta_next_ref
  126.1 9.6 %all-gather.2.cloned.1.call-done = bf16[1024,1536]{1,0:T(8,128)(2,1)} async-done(((bf16[256,1536]{1,0:T(8,128)(2,1)}), bf16[1024,1536]{1,0:T(8,128)(2,1)}) %all-gather.2.cloned.1.call-update) | async-done | bytes 3145744 | tf_op jit(solution)/shard_map/all_gather | solution.py:999
  135.7 8.5 %multiply_reduce_fusion = (f32[1024]{0:T(1024)}, f32[1024,768]{1,0:T(8,128)}) fusion(f32[1024,768]{1,0:T(8,128)} %get-tuple-element.58, f32[768]{0:T(1024)S(1)} %copy-done.9, bf16[1024,1536]{1,0:T(8,128)(2,1)} %all-gather.2.cloned.1.call-done, bf16[1536,768]{1,0:T(8,128)(2,1)} %get-tuple-element.60), kind=kOutput, calls=%fused_computation.9 | convolution fusion | flops 2418277376 | bytes 11803648 | tf_op jit(solution)/shard_map/dot_general | solution.py:977
  144.2 7.0 %dot_sum.1.dots_ref = f32[1,1024]{1,0:T(1,128)} custom-call(f32[1,1024]{1,0:T(1,128)} %bitcast.74), custom_call_target="tpu_custom_call" | custom-call | tf_op jit(solution)/shard_map/dot_sum/pallas_call | solution.py:678
  151.2 26.6 %ssm_backward.1 = (bf16[1024,1664]{1,0:T(8,128)(2,1)}, bf16[1024,256]{1,0:T(8,128)(2,1)}, f32[8,1024]{1,0:T(8,128)}, f32[8,256]{1,0:T(8,128)}, f32[8,768]{1,0:T(8,128)}, /*index=5*/f32[8,768]{1,0:T(8,128)}) custom-call(f32[1024,1664]{1,0:T(8,128)} %fusion.28.gate_ref.conv_ref.dt_ref.halo_ref, f32[1024,1664]{1,0:T(8,128)} %fusion.28.gate_ref.conv_ref.dt_ref.halo_ref, ...), custom_call_target="tpu_custom_call" | custom-call | tf_op jit(solution)/shard_map/ssm_backward/pallas_call | solution.py:344
  177.9 8.9 %fusion.30 = f32[1024,1536]{1,0:T(8,128)S(1)} fusion(bf16[1024,1664]{1,0:T(8,128)(2,1)} %get-tuple-element.68, bf16[1536,1664]{1,0:T(8,128)(2,1)} %get-tuple-element.56), kind=kOutput, calls=%fused_computation.51 | convolution fusion | flops 5234491392 | bytes 14811136 | tf_op jit(solution)/shard_map/dot_general | solution.py:977
  186.8 2.9 %fusion.4 = (f32[1536]{0:T(1024)S(1)}, bf16[1024,1536]{1,0:T(8,128)(2,1)}) fusion(bf16[1024,1536]{1,0:T(8,128)(2,1)S(1)} %copy-done, f32[1024]{0:T(1024)S(1)} %add_rsqrt_fusion, f32[1024,1536]{1,0:T(8,128)S(1)} %fusion.30, bf16[1024,256]{1,0:T(8,128)(2,1)S(1)} %copy-done.4, bf16[1536,256]{1,0:T(8,128)(2,1)S(1)} %bitcast.55), kind=kOutput, calls=%fused_computation.7 | convolution fusion | flops 816314880 | bytes 13903872 | tf_op jit(solution)/shard_map/dot_general | solution.py:977
  189.8 0.0 reduce-scatter.5.cloned.1.call-update
  189.8 0.9 fusion.19
  190.7 0.7 reshape.137.gain_ref
  191.4 0.7 slice.66
  192.1 0.7 slice.67
  192.8 0.7 slice.68
  193.6 9.9 %fusion.24.ga_ref = bf16[1536,1664]{1,0:T(8,128)(2,1)} fusion(bf16[1024,1664]{1,0:T(8,128)(2,1)} %get-tuple-element.68, bf16[1024,1536]{1,0:T(8,128)(2,1)S(1)} %copy-done, f32[1536]{0:T(1024)S(1)} %reshape.138, f32[1024]{0:T(1024)S(1)} %add_rsqrt_fusion), kind=kOutput, calls=%fused_computation.48 | convolution fusion | flops 5240782848 | bytes 11675648 | tf_op jit(solution)/shard_map/dot_general | solution.py:977
  203.6 1.3 concatenate.36.small_ref
  204.9 3.5 %fusion.22.gb_ref = bf16[1536,256]{1,0:T(8,128)(2,1)} fusion(bf16[1024,256]{1,0:T(8,128)(2,1)} %get-tuple-element.69, bf16[1024,1536]{1,0:T(8,128)(2,1)S(1)} %copy-done, f32[1536]{0:T(1024)S(1)} %reshape.138, f32[1024]{0:T(1024)S(1)} %add_rsqrt_fusion), kind=kOutput, calls=%fused_computation.47 | convolution fusion | flops 811597824 | bytes 4466688 | tf_op jit(solution)/shard_map/dot_general | solution.py:977
  208.4 4.3 %fusion.20.go_ref = bf16[1536,768]{1,0:T(8,128)(2,1)} fusion(bf16[1024,1536]{1,0:T(8,128)(2,1)S(1)} %copy-done.15, f32[1024,768]{1,0:T(8,128)S(1)} %copy-done.16, f32[768]{0:T(1024)S(1)} %copy-done.9, f32[1024]{0:T(1024)S(1)} %bitcast.64), kind=kOutput, calls=%fused_computation.45 | convolution fusion | flops 2418278400 | bytes 8657920 | tf_op jit(solution)/shard_map/dot_general | solution.py:977
  212.6 49.9 %exit_reduce.1 = (f32[192,1664]{1,0:T(8,128)}, f32[192,768]{1,0:T(8,128)}, f32[48,256]{1,0:T(8,128)}, f32[16,1536]{1,0:T(8,128)}, f32[8,1536]{1,0:T(8,128)}) custom-call(bf16[1536,1664]{1,0:T(8,128)(2,1)} %fusion.24.ga_ref, bf16[1536,768]{1,0:T(8,128)(2,1)} %fusion.20.go_ref, bf16[1536,256]{1,0:T(8,128)(2,1)} %fusion.22.gb_ref, f32[16,1536]{1,0:T(8,128)} %concatenate.36.small_ref), custom_call_target="tpu_custom_call" | custom-call | tf_op jit(solution)/shard_map/exit_reduce/pallas_call | solution.py:881
  262.5 0.0 copy-start.3
  262.5 0.9 slice.70
  263.4 0.6 dynamic-slice_bitcast_fusion
  264.0 2.2 reduce-scatter.5.cloned.1.call-done.d_own_ref
  266.2 6.4 %finish.1 = (bf16[256,1536]{1,0:T(8,128)(2,1)}, f32[256,1536]{1,0:T(8,128)}, f32[192,2,768]{2,1,0:T(2,128)}, f32[48,256]{1,0:T(8,128)}, f32[12,192]{1,0:T(8,128)...) custom-call(bf16[256,1536]{1,0:T(8,128)(2,1)} %tok_ref.3, ...), custom_call_target="tpu_custom_call" | custom-call | tf_op jit(solution)/shard_map/finish/pallas_call | solution.py:961
  272.6 1.3 reduce.2
  273.9 1.3 reduce.3
  275.2 0.8 copy.65
  (61 shorter events, 0.2 us)
Async XLA Ops:
  7.2 66.0 %copy-start.5 = (s32[1,1024]{1,0:T(1,128)S(1)}, s32[1,1024]{1,0:T(1,128)}, u32[]{:S(2)}) copy-start(s32[1,1024]{1,0:T(1,128)} %param.17) | copy-start | bytes 12292
  7.2 66.1 %copy-start.9 = (f32[768]{0:T(1024)S(1)}, f32[768]{0:T(1024)}, u32[]{:S(2)}) copy-start(f32[768]{0:T(1024)} %param.30) | copy-start | bytes 9220
  7.2 66.1 %copy-start.17 = (f32[12]{0:T(128)S(1)}, f32[12]{0:T(128)}, u32[]{:S(2)}) copy-start(f32[12]{0:T(128)} %param.28) | copy-start | bytes 148
  7.2 66.2 %copy-start.13 = (f32[12]{0:T(128)S(1)}, f32[12]{0:T(128)}, u32[]{:S(2)}) copy-start(f32[12]{0:T(128)} %param.27) | copy-start | bytes 148
  7.2 66.3 %copy-start.14 = (f32[12]{0:T(128)S(1)}, f32[12]{0:T(128)}, u32[]{:S(2)}) copy-start(f32[12]{0:T(128)} %param.29) | copy-start | bytes 148
  7.2 69.4 %copy-start.12 = (f32[256]{0:T(256)S(1)}, f32[256]{0:T(256)}, u32[]{:S(2)}) copy-start(f32[256]{0:T(256)} %param.26) | copy-start | bytes 3076
  7.2 69.4 %copy-start.10 = (f32[768]{0:T(1024)S(1)}, f32[768]{0:T(1024)}, u32[]{:S(2)}) copy-start(f32[768]{0:T(1024)} %param.24) | copy-start | bytes 9220
  7.3 69.4 %copy-start.11 = (f32[4,256]{1,0:T(4,128)S(1)}, f32[4,256]{1,0:T(4,128)}, u32[]{:S(2)}) copy-start(f32[4,256]{1,0:T(4,128)} %param.25) | copy-start | bytes 12292
  7.3 69.4 %copy-start.8 = (f32[4,768]{1,0:T(4,128)S(1)}, f32[4,768]{1,0:T(4,128)}, u32[]{:S(2)}) copy-start(f32[4,768]{1,0:T(4,128)} %param.23) | copy-start | bytes 36868
  7.3 128.5 %all-gather.2.cloned.1.call-start = ((), (), s32[]{:S(2)}) async-start(), calls=%async_computation.3 | async-start | bytes 3932160 | tf_op jit(solution)/shard_map/all_gather | solution.py:999
  73.1 7.9 %copy-start = (bf16[1024,1536]{1,0:T(8,128)(2,1)S(1)}, bf16[1024,1536]{1,0:T(8,128)(2,1)}, u32[]{:S(2)}) copy-start(bf16[1024,1536]{1,0:T(8,128)(2,1)} %get-tuple-element.55) | copy-start | bytes 9437188
  73.1 190.9 %reduce-scatter.3.cloned.1.call-start = ((), (), s32[]{:S(2)}) async-start(), calls=%async_computation.2 | async-start | bytes 3932160 | tf_op jit(solution)/shard_map/reduce_scatter | solution.py:1029
  78.0 3.0 %copy-start.1 = (bf16[8,4,48,256]{3,2,1,0:T(8,128)(2,1)S(1)}, bf16[8,4,48,256]{3,2,1,0:T(8,128)(2,1)}, u32[]{:S(2)}) copy-start(bf16[8,4,48,256]{3,2,1,0:T(8,128)(2,1)} %get-tuple-element.57) | copy-start | bytes 2359300
  78.0 5.0 %slice-start = ((s8[5111808]{0:T(1024)(128)(4,1)}), s8[4194304]{0:T(1024)(128)(4,1)S(1)}, s32[]{:S(2)}) async-start(s8[5111808]{0:T(1024)(128)(4,1)} %bitcast.77), calls=%async_computation.5 | async-start | bytes 8388608
  81.0 2.0 slice-start.1
  125.0 141.2 %reduce-scatter.5.cloned.1.call-start = ((), (), s32[]{:S(2)}) async-start(), calls=%async_computation.4 | async-start | bytes 3932160 | tf_op jit(solution)/shard_map/reduce_scatter | solution.py:1053
  177.8 9.0 %copy-start.2 = (bf16[8,4,48,256]{3,2,1,0:T(8,128)(2,1)S(1)}, bf16[8,4,48,256]{3,2,1,0:T(8,128)(2,1)}, u32[]{:S(2)}) copy-start(bf16[8,4,48,256]{3,2,1,0:T(8,128)(2,1)} %get-tuple-element.57) | copy-start | bytes 2359300
  177.8 9.0 %copy-start.4 = (bf16[1024,256]{1,0:T(8,128)(2,1)S(1)}, bf16[1024,256]{1,0:T(8,128)(2,1)}, u32[]{:S(2)}) copy-start(bf16[1024,256]{1,0:T(8,128)(2,1)} %get-tuple-element.69) | copy-start | bytes 1572868
  189.8 1.6 copy-start.6
  204.9 3.5 %copy-start.7 = (f32[1,1024]{1,0:T(1,128)S(1)}, f32[1,1024]{1,0:T(1,128)}, u32[]{:S(2)}) copy-start(f32[1,1024]{1,0:T(1,128)} %rms_sum.1.rms_ref) | copy-start | bytes 12292
  204.9 3.5 %copy-start.15 = (bf16[1024,1536]{1,0:T(8,128)(2,1)S(1)}, bf16[1024,1536]{1,0:T(8,128)(2,1)}, u32[]{:S(2)}) copy-start(bf16[1024,1536]{1,0:T(8,128)(2,1)} %all-gather.2.cloned.1.call-done) | copy-start | bytes 9437188
  204.9 3.5 %copy-start.16 = (f32[1024,768]{1,0:T(8,128)S(1)}, f32[1024,768]{1,0:T(8,128)}, u32[]{:S(2)}) copy-start(f32[1024,768]{1,0:T(8,128)} %get-tuple-element.58) | copy-start | bytes 9437188
  262.5 12.7 %copy-start.3 = (f32[192,768]{1,0:T(8,128)S(1)}, f32[192,768]{1,0:T(8,128)}, u32[]{:S(2)}) copy-start(f32[192,768]{1,0:T(8,128)} %get-tuple-element.92) | copy-start | bytes 1769476
Sparse Core Ops, SparseCore 0:
  73.2 62.4 all-gather.1
  138.0 59.2 reduce-scatter.2
  199.6 66.5 reduce-scatter.4

commit v2 on v1

--- a/solution.py
+++ b/solution.py
@@ -194,7 +194,7 @@
     inner,
     gate_ref, conv_ref, halo_ref, bc_ref, bc_halo_ref, dt_ref, meta_ref, meta_next_ref, seg_row_ref,
     params_ref, core_ref, d_normed_ref, rms_ref, dots_ref, states_ref, pre_ref, lanes_ref, save_ref,
-    dz_ref, dbc_ref, gconv_ref, ghead_ref, ggain_ref, gskip_ref,
+    dz_ref, packed_ref,
     window, d_window, d_state,
 ):
     width = conv_ref.shape[1]
@@ -205,10 +205,7 @@
     def _():
         d_window[pl.ds(CHUNK, HALO), :] = jnp.zeros((HALO, d_window.shape[1]), F32)
         d_state[...] = jnp.zeros_like(d_state)
-        gconv_ref[...] = jnp.zeros_like(gconv_ref)
-        ghead_ref[...] = jnp.zeros_like(ghead_ref)
-        ggain_ref[...] = jnp.zeros_like(ggain_ref)
-        gskip_ref[...] = jnp.zeros_like(gskip_ref)
+        packed_ref[...] = jnp.zeros_like(packed_ref)
 
     @pl.when(place > 0)
     def _():
@@ -252,7 +249,7 @@
     d_gated = gate_rms * params_ref[8:9, :width] * d_normed - gated * (
         (gate_rms * gate_rms * gate_rms) * inner_dot / inner
     )
-    ggain_ref[0:1] += jnp.sum(d_normed * gated * gate_rms, 0, keepdims=True)
+    packed_ref[5:6, :width] += jnp.sum(d_normed * gated * gate_rms, 0, keepdims=True)
     d_core = d_gated * gate_act
     dz_ref[:, :width] = (d_gated * core * (gate_sig * (1.0 + gate * (1.0 - gate_sig)))).astype(BF16)
 
@@ -299,10 +296,10 @@
     d_dt = d_step * slope_dt
     head_lane = lax.broadcasted_iota(jnp.int32, d_dt.shape, 1) < width // HEAD_DIM
     d_dt = jnp.where(head_lane, d_dt, 0.0)
-    dz_ref[:, 2 * width :] = d_dt.astype(BF16)
-    ghead_ref[0:1, :LANES] += jnp.sum(d_dt, 0, keepdims=True)
-    ghead_ref[0:1, LANES:] += jnp.sum(d_rate * (step * params_ref[6:7, :LANES]), 0, keepdims=True)
-    gskip_ref[0:1] += jnp.sum(d_core * mixer_in, 0, keepdims=True)
+    dz_ref[:, 2 * width : 2 * width + LANES] = d_dt.astype(BF16)
+    packed_ref[6:7, :LANES] += jnp.sum(d_dt, 0, keepdims=True)
+    packed_ref[6:7, LANES : 2 * LANES] += jnp.sum(d_rate * (step * params_ref[6:7, :LANES]), 0, keepdims=True)
+    packed_ref[7:8, :width] += jnp.sum(d_core * mixer_in, 0, keepdims=True)
     d_state[...] = passing * d_outgoing + mm(output_mat, scaled_d, TN)
 
     d_mixer = d_weighted * step_l + d_core * params_ref[7:8, :width]
@@ -313,23 +310,26 @@
     d_window[pl.ds(0, CHUNK), width : width + STATE] = d_pre_b
     d_window[pl.ds(0, CHUNK), width + STATE :] = d_pre_c
     d_pre = d_window[pl.ds(0, CHUNK), :]
-    gconv_ref[4:5] += jnp.sum(d_pre, 0, keepdims=True)
-    gconv_ref[0:1] += jnp.sum(d_pre * window[pl.ds(HALO, CHUNK), :], 0, keepdims=True)
+    taps_seen = [jnp.sum(d_pre * window[pl.ds(HALO, CHUNK), :], 0, keepdims=True)]
     total = params_ref[0:1] * d_pre
     for back in (1, 2, 3):
-        gconv_ref[back : back + 1] += jnp.sum(
-            d_pre * (window[pl.ds(HALO - back, CHUNK), :] * meta[:, back : back + 1]), 0, keepdims=True
+        taps_seen.append(
+            jnp.sum(d_pre * (window[pl.ds(HALO - back, CHUNK), :] * meta[:, back : back + 1]), 0, keepdims=True)
         )
         total = total + params_ref[back : back + 1] * (
             d_window[pl.ds(back, CHUNK), :] * meta_next_ref[:, back : back + 1]
         )
     dz_ref[:, width : 2 * width] = total[:, :width].astype(BF16)
-    dbc_ref[...] = total[:, width:].astype(BF16)
+    dz_ref[:, 2 * width + LANES :] = total[:, width:].astype(BF16)
+    taps_seen.append(jnp.sum(d_pre, 0, keepdims=True))
+    for place_at, seen in enumerate(taps_seen):
+        packed_ref[place_at : place_at + 1, :width] += seen[:, :width]
+        packed_ref[9 + place_at : 10 + place_at, : 2 * STATE] += seen[:, width:]
 
 
 def ssm_backward(
     inner, projected, bc_pre, meta, meta_next, seg_row, params, core, d_normed, rms, dots, states,
-    pre, lanes, save,
+    pre, lanes, save, model,
 ):
     length, width = core.shape
     chunks = length // CHUNK
@@ -355,16 +355,11 @@
             row(channels), row(3 * width), row(2 * LANES),
         ],
         out_specs=[
-            row(2 * width + LANES), row(2 * STATE),
-            whole(8, channels), whole(8, 2 * LANES), whole(8, width), whole(8, width),
+            row(2 * width + LANES + 2 * STATE), whole(16, model),
         ],
         out_shape=[
-            jax.ShapeDtypeStruct((length, 2 * width + LANES), BF16),
-            jax.ShapeDtypeStruct((length, 2 * STATE), BF16),
-            jax.ShapeDtypeStruct((8, channels), F32),
-            jax.ShapeDtypeStruct((8, 2 * LANES), F32),
-            jax.ShapeDtypeStruct((8, width), F32),
-            jax.ShapeDtypeStruct((8, width), F32),
+            jax.ShapeDtypeStruct((length, 2 * width + LANES + 2 * STATE), BF16),
+            jax.ShapeDtypeStruct((16, model), F32),
         ],
         scratch_shapes=[
             pltpu.VMEM((CHUNK + HALO, channels), F32),
@@ -703,9 +698,9 @@
 
 def exit_kernel(
     tensor_size, dp_size,
-    ga_ref, go_ref, gb_ref, small_ref,
+    ga_ref, go_ref, small_ref,
     sa_ref, so_ref, sb_ref, plane_sum_ref, all_sum_ref,
-    near_a, near_o, near_b, far_a, far_o, far_b, mid_b, b_slots, pair_ref, plane_slots, line_slots,
+    near_a, near_o, far_a, far_o, mid_b, b_slots, pair_ref, line_ref, plane_slots, line_slots,
     near_send, near_recv, far_send, far_recv,
     b_send, b_recv, plane_send, plane_recv, line_send, line_recv,
 ):
@@ -715,9 +710,9 @@
     sibling = {"dp": plane + 1 - 2 * core}
     greet(tensor_size, dp_size)
 
-    grads = [(ga_ref, near_a, far_a), (go_ref, near_o, far_o), (gb_ref, near_b, far_b)]
+    grads = [(ga_ref, near_a, far_a), (go_ref, near_o, far_o)]
     order = [3, 1, 2, 0] if relay else list(range(1, chips)) + [0]
-    arrays = (2, 0, 1)
+    arrays = (0, 1)
 
     def device(offset, side):
         return 2 * flip(chip, offset) + side
@@ -747,7 +742,7 @@
 
     def small_line(offset):
         return remote(
-            plane_sum_ref.at[pl.ds(8, 8)], line_slots.at[offset], line_send.at[offset], line_recv.at[offset],
+            line_ref, line_slots.at[offset], line_send.at[offset], line_recv.at[offset],
             {"tensor": lax.rem(line + offset, tensor_size)},
         )
 
@@ -815,12 +810,17 @@
         small_plane(offset).wait_recv()
         total = total + plane_slots[offset]
     plane_sum_ref[...] = total
+    lanes = line_ref.shape[1]
+    line_ref[...] = jnp.zeros_like(line_ref)
+    for piece in range(4):
+        line_ref[piece : piece + 1] = total[8:9, piece * lanes : (piece + 1) * lanes]
+    line_ref[4:9, : 2 * STATE] = total[9:14, : 2 * STATE]
     for offset in range(1, tensor_size):
         small_line(offset).start()
 
     direct = (1, 2) if relay else tuple(range(1, chips))
     block = sb_ref.shape[0]
-    for which, out in ((2, mid_b), (0, sa_ref), (1, so_ref)):
+    for which, out in ((0, sa_ref), (1, so_ref)):
         _, near, far = grads[which]
         for offset in direct:
             for half in (0, 1):
@@ -833,7 +833,13 @@
             out[pl.ds(at, BAND), :] = total
 
         add_rows(put, terms, near.shape[1])
-        if which == 2:
+        if which == 0:
+            wide = sb_ref.shape[1]
+            own_b = sa_ref.shape[0] // tensor_size
+            for j in range(tensor_size):
+                mid_b[pl.ds(j * block, own_b), :] = sa_ref[
+                    pl.ds(j * own_b, own_b), sa_ref.shape[1] - wide :
+                ].astype(BF16)
             b_copies = [
                 remote(
                     mid_b.at[rows_at(lax.rem(line + offset, tensor_size), block)], b_slots.at[offset],
@@ -844,19 +850,19 @@
             for copy in b_copies:
                 copy.start()
 
-    total = plane_sum_ref[8:]
+    total = line_ref[...]
     for offset in range(1, tensor_size):
         small_line(offset).wait_recv()
         total = total + line_slots[offset]
     all_sum_ref[...] = total
 
-    total = mid_b[rows_at(line, block), :]
+    total = mid_b[rows_at(line, block), :].astype(F32)
     for offset, copy in enumerate(b_copies, 1):
         copy.wait_recv()
-        total = total + b_slots[offset]
+        total = total + b_slots[offset].astype(F32)
     sb_ref[...] = total
 
-    for which in range(3):
+    for which in arrays:
         for offset in range(chips):
             near_copy(which, offset).wait_send()
             if offset:
@@ -871,36 +877,37 @@
         small_line(offset).wait_send()
 
 
-def leave(tensor_size, dp_size, ga, go, gb, small):
+def leave(tensor_size, dp_size, block, wide, ga, go, small):
     vmem = pl.BlockSpec(memory_space=pltpu.VMEM)
     dma = pltpu.SemaphoreType.DMA
     chips = dp_size // 2
-    ra, ro, rb = (g.shape[0] // dp_size for g in (ga, go, gb))
-    block = rb // tensor_size
+    packed_line = (16, small.shape[1] // 4)
+    ra, ro = ga.shape[0] // dp_size, go.shape[0] // dp_size
     slots = lambda n, r, c, t=BF16: pltpu.VMEM((n, r, c), t)
     return pl.pallas_call(
         functools.partial(exit_kernel, tensor_size, dp_size),
-        in_specs=[vmem] * 4,
+        in_specs=[vmem] * 3,
         out_specs=[vmem] * 5,
         out_shape=[
             jax.ShapeDtypeStruct((ra, ga.shape[1]), F32),
             jax.ShapeDtypeStruct((ro, go.shape[1]), F32),
-            jax.ShapeDtypeStruct((block, gb.shape[1]), F32),
+            jax.ShapeDtypeStruct((block, wide), F32),
             jax.ShapeDtypeStruct(small.shape, F32),
-            jax.ShapeDtypeStruct((8, small.shape[1]), F32),
+            jax.ShapeDtypeStruct(packed_line, F32),
         ],
         scratch_shapes=[
-            slots(chips, ra, ga.shape[1]), slots(chips, ro, go.shape[1]), slots(chips, rb, gb.shape[1]),
-            slots(chips, ra, ga.shape[1]), slots(chips, ro, go.shape[1]), slots(chips, rb, gb.shape[1]),
-            pltpu.VMEM((rb, gb.shape[1]), F32), slots(tensor_size, block, gb.shape[1], F32),
-            pltpu.VMEM(small.shape, F32), slots(chips, *small.shape, F32), slots(tensor_size, 8, small.shape[1], F32),
-            dma((3, chips)), dma((3, chips)), dma((3, chips, 2)), dma((3, chips, 2)),
+            slots(chips, ra, ga.shape[1]), slots(chips, ro, go.shape[1]),
+            slots(chips, ra, ga.shape[1]), slots(chips, ro, go.shape[1]),
+            pltpu.VMEM((tensor_size * block, wide), BF16), slots(tensor_size, block, wide),
+            pltpu.VMEM(small.shape, F32), pltpu.VMEM(packed_line, F32),
+            slots(chips, *small.shape, F32), slots(tensor_size, *packed_line, F32),
+            dma((2, chips)), dma((2, chips)), dma((2, chips, 2)), dma((2, chips, 2)),
             dma((tensor_size,)), dma((tensor_size,)), dma((chips,)), dma((chips,)),
             dma((tensor_size,)), dma((tensor_size,)),
         ],
         compiler_params=pltpu.CompilerParams(collective_id=2, has_side_effects=True, vmem_limit_bytes=60 * MIB),
         name="exit_reduce",
-    )(ga, go, gb, small)
+    )(ga, go, small)
 
 
 STEPS = 4
@@ -936,12 +943,13 @@
         heads = dtb_ref.shape[1]
         gdt_ref[...] = dt_ref[...].T[:heads]
         cxw_ref[...] = plane_ref[:4, :width]
-        cxb_ref[...] = plane_ref[4:5, :width]
-        gate_ref[...] = plane_ref[5:6, :width]
+        for i in range(width // LANES):
+            cxb_ref[i : i + 1] = plane_ref[4:5, i * LANES : (i + 1) * LANES]
+            gate_ref[i : i + 1] = plane_ref[5:6, i * LANES : (i + 1) * LANES]
         dtb_ref[...] = plane_ref[6:7, :heads]
         alog_ref[...] = plane_ref[6:7, LANES : LANES + heads]
-        cbw_ref[...] = all_ref[1:5, : 2 * STATE]
-        cbb_ref[...] = all_ref[5:6, : 2 * STATE]
+        cbw_ref[...] = all_ref[4:8, : 2 * STATE]
+        cbb_ref[...] = all_ref[8:9, : 2 * STATE]
         per_head = gather_heads(jnp.broadcast_to(plane_ref[7:8, :width], (8, width)), head_expand(width))
         skip_ref[...] = per_head[0:1, :heads]
 
@@ -952,8 +960,8 @@
     fixed = lambda a: pl.BlockSpec(a, lambda i: (0, 0))
     shapes = [
         (tokens.shape, BF16), (tokens.shape, F32), ((sa.shape[0], 2, width), F32), ((bc_rows, sb.shape[1]), F32),
-        ((heads, sa.shape[0]), F32), ((4, width), F32), ((1, width), F32), ((4, 2 * STATE), F32), ((1, 2 * STATE), F32),
-        ((1, heads), F32), ((1, heads), F32), ((1, heads), F32), ((1, width), F32),
+        ((heads, sa.shape[0]), F32), ((4, width), F32), ((width // LANES, LANES), F32), ((4, 2 * STATE), F32), ((1, 2 * STATE), F32),
+        ((1, heads), F32), ((1, heads), F32), ((1, heads), F32), ((width // LANES, LANES), F32),
     ]
     kinds = [row, row, row] + [fixed] * 10
     args = (tokens, cotangent, gain, mixed, d_own, sa, sa, sb, plane_sum, all_sum)
@@ -1027,32 +1035,25 @@
     normed_out = (gated * rms[0][:, None] * gate_row).astype(BF16)
     mixed = dot(normed_out, wo_all, ((1,), (1,)), BF16)
     mixed_own = lax.psum_scatter(mixed, "tensor", scatter_dimension=0, tiled=True)
-    d_out, mixed = lax.optimization_barrier((d_out, mixed))
+    weights = jnp.concatenate([wa_all, wb_all], 1)
+    d_out, mixed, weights = lax.optimization_barrier((d_out, mixed, weights))
     d_normed = dot(d_out, wo_all, ((1,), (0,)))
     inner_part = jnp.sum(gated * gate_row * d_normed, -1)[None]
-    dots = stat_sum(tensor_size, None, inner_part, 3)
-
-    dz, dbc, gconv, ghead, ggain, gskip = ssm_backward(
-        inner, projected, bc_pre, meta, meta_next, seg_row, params, core, d_normed, rms, dots, states, pre, lanes, small_save
+    dots = inner_part
+    for step in range(1, tensor_size):
+        dots = dots + lax.ppermute(inner_part, "tensor", [(i, (i + step) % tensor_size) for i in range(tensor_size)])
+    go = dot(d_out, normed_out, ((0,), (0,)), BF16)
+
+    dz, packed = ssm_backward(
+        inner, projected, bc_pre, meta, meta_next, seg_row, params, core, d_normed, rms, dots, states, pre, lanes, small_save, model
     )
-    go = dot(d_out, normed_out, ((0,), (0,)), BF16)
-    part = (dot(dz, wa_all, ((1,), (1,))) + dot(dbc, wb_all, ((1,), (1,)))).astype(BF16)
+    part = dot(dz, weights, ((1,), (1,)), BF16)
     ga = dot(normed_in, dz, ((0,), (0,)), BF16)
-    gb = dot(normed_in, dbc, ((0,), (0,)), BF16)
-    gb = jnp.pad(
-        gb.reshape(dp_size * tensor_size, bc_rows, 2 * STATE), ((0, 0), (0, bc_padded - bc_rows), (0, 0))
-    ).reshape(dp_size * tensor_size * bc_padded, 2 * STATE)
     gnorm = jnp.sum(part.astype(F32) * x_all * inv_all, 0)[None]
-    packed = jnp.concatenate(
-        [
-            pad_lanes(gconv[:5, :width], model), pad_lanes(ggain[:1], model), pad_lanes(ghead[:1], model),
-            pad_lanes(gskip[:1], model), gnorm, pad_lanes(gconv[:5, width:], model), jnp.zeros((2, model), F32),
-        ],
-        0,
-    )
+    packed = lax.dynamic_update_slice(packed, gnorm, (8, 0))
     d_own = lax.psum_scatter(part, "tensor", scatter_dimension=0, tiled=True)
     ga, part = lax.optimization_barrier((ga, part))
-    sa, so, sb, plane_sum, all_sum = leave(tensor_size, dp_size, ga, go, gb, packed)
+    sa, so, sb, plane_sum, all_sum = leave(tensor_size, dp_size, bc_padded, 2 * STATE, ga, go, packed)
     layer_out, grad_tokens, gzx, gbc, gdt, cxw, cxb, cbw, cbb, dtb, alog, gsk, ggate = finish(
         width, bc_rows, heads_here, tokens, cotangent, gain, mixed_own, d_own, sa, sb, plane_sum, all_sum
     )
@@ -1061,8 +1062,8 @@
     return (
         layer_out,
         grad_tokens,
-        lax.dynamic_slice(all_sum[0], (place * own_gain,), (own_gain,)),
-        gzx, gbc, gdt.T, cxw, cxb[0], cbw, cbb[0], dtb[0], alog[0], gsk[0], ggate[0], so.T,
+        lax.dynamic_slice(all_sum[:4].reshape(model), (place * own_gain,), (own_gain,)),
+        gzx, gbc, gdt.T, cxw, cxb.reshape(width), cbw, cbb[0], dtb[0], alog[0], gsk[0], ggate.reshape(width), so.T,
     )
 
 

time: 283 us -> 278 us (0.982)
  Pallas kernels: 177 us -> 172 us
  other arithmetic: 8.99 us -> 12.7 us
  starting transfers between devices: 0.12 us -> 3.17 us
    pallas_call x2 -> x1, Pallas kernels: 14 us -> 7.01 us  [stat_sum(): pl.pallas_call(functools.partial(stat_kernel, tensor_size, inner), in_spe...]
    concatenate x0 -> x1, other arithmetic: none -> 5.68 us  [body(): weights = jnp.concatenate([wa_all, wb_all], 1)]
    all_gather x1, waiting for transfers between devices: 9.63 us -> 5.02 us  [body(): d_out = lax.all_gather(cot_late, 'tensor', axis=0, tiled=True)]
    ppermute x0 -> x3, starting transfers between devices: none -> 3.04 us  [body(): lax.ppermute(inner_part, 'tensor', [(i, (i + step) % tensor_size) for i i...]
    dot_general x9 -> x7, matrix products: 55 us -> 52.5 us  [dot(): return lax.dot_general(a, b, (dims, ((), ())), preferred_element_type=out)]
  transfers between devices with their start and end apart: 3 -> 6, of which waited for: 2 -> 5; matrix products, arithmetic and copies ran while one was open for 25% -> 26% of each run, Pallas kernels for 39% -> 38%
where the time goes in v2:
time: 278 us; the launch traced here: 277 us
  Pallas kernels  172 us (62%)
  matrix products  52.5 us (19%)
  between operations  14.1 us (5%)
  local copies, waits for them, and re-layouts  13 us (5%)
  other arithmetic  12.7 us (5%)
  waiting for transfers between devices  9.1 us (3%)
  starting transfers between devices  3.17 us (1%)
    pallas_call x1, Pallas kernels, entry(): pl.pallas_call(functools.partial(entry_kernel, tensor_size, dp_size), in_...  61.7 us
    dot_general x7, matrix products, dot(): return lax.dot_general(a, b, (dims, ((), ())), preferred_element_type=out)  52.5 us
    pallas_call x1, Pallas kernels, leave(): pl.pallas_call(functools.partial(exit_kernel, tensor_size, dp_size), in_s...  51.4 us
    pallas_call x1, Pallas kernels, ssm_backward(): pl.pallas_call(functools.partial(backward_kernel, inner), grid=(chunks,),...  27.2 us
    pallas_call x1, Pallas kernels, ssm_forward(): pl.pallas_call(forward_kernel, grid=(chunks,), in_specs=[row(width), row(...  18.6 us
    pallas_call x1, Pallas kernels, stat_sum(): pl.pallas_call(functools.partial(stat_kernel, tensor_size, inner), in_spe...  7.01 us
    pallas_call x1, Pallas kernels, finish(): pl.pallas_call(functools.partial(finish_kernel, width, bc_rows), grid=(ST...  6.51 us
    concatenate x1, other arithmetic, body(): weights = jnp.concatenate([wa_all, wb_all], 1)  5.68 us
  transfers between devices with their start and end apart: 6, of which 5 were waited for; matrix products, arithmetic and copies ran while one was open for 26% of the time, Pallas kernels for 38%

profile of v2, /device:TPU:0, one launch (start us, length us, event | category | flops | bytes accessed | tf_op | source)
XLA Modules:
  0.0 276.9 jit_solution(14092733729728359223)
XLA Ops:
  7.3 0.0 all-gather.2.cloned.1.call-start
  7.3 0.7 pad_bitcast_fusion
  8.0 0.8 copy.52
  8.8 1.1 copy.63
  9.9 0.9 fusion.6.wa_ref
  10.8 0.6 broadcast_in_dim.36.gain_ref
  11.4 61.7 %entry_gather.1 = (bf16[1024,1536]{1,0:T(8,128)(2,1)}, bf16[1536,1664]{1,0:T(8,128)(2,1)}, bf16[1536,768]{1,0:T(8,128)(2,1)}, bf16[8,4,48,256]{3,2,1,0:T(8,128)(2,1)}, bf16[8,4,16,128]{3,2,1,0:T(8,128)(2,1)}) custom-call(bf16[256,1536]{1,0:T(8,128)(2,1)} %tok_ref.3, bf16[192,1664]{1,0:T(8,128)(2,1)} %fusion.6.wa_ref, bf16[192,768]{1,0:T(8,128)(2,1)} %bitcast.57, ...), custom_call_target="tpu_custom_call" | custom-call | tf_op jit(solution)/shard_map/entry_gather/pallas_call | solution.py:623
  73.1 0.0 all-gather.2.cloned.1.call-update
  73.1 0.0 reduce-scatter.3.cloned.1.call-start
  73.2 0.1 slice.41
  73.2 0.1 slice.45
  73.3 0.0 copy-done.6
  73.4 0.1 copy.61
  73.5 0.1 copy.62
  73.6 0.1 broadcast_in_dim.39
  73.6 0.1 broadcast_in_dim_reshape.3
  73.7 0.1 add_bitcast_fusion
  73.8 0.6 convert_bitcast_fusion
  74.4 0.1 eq.59
  74.5 0.1 eq.66
  74.6 0.1 fusion.13
  74.6 0.1 stack.58
  74.7 1.0 copy.55.meta_ref
  75.7 0.8 slice_convert_fusion
  76.6 0.1 reshape.147
  76.6 0.0 copy-done.7
  76.7 1.3 concatenate.34.params_ref
  78.0 3.0 %fusion = f32[1024]{0:T(1024)S(1)} fusion(bf16[1024,1536]{1,0:T(8,128)(2,1)} %get-tuple-element.52), kind=kLoop, calls=%fused_computation.3 | loop fusion | flops 4717568 | bytes 3149824 | tf_op jit(solution)/shard_map/reduce_sum | solution.py:1027
  81.0 0.0 slice-start.1
  81.0 2.0 fusion.24.bc_ref.bc_halo_ref
  83.0 0.0 slice-done
  83.0 8.0 %fusion.26.gate_ref.conv_ref.dt_ref.halo_ref = f32[1024,1664]{1,0:T(8,128)} fusion(bf16[1536,1664]{1,0:T(8,128)(2,1)S(1)} %bitcast.51, bf16[1024,1536]{1,0:T(8,128)(2,1)S(1)} %copy-done, f32[1536]{0:T(1024)S(1)} %reshape.147, f32[1024]{0:T(1024)S(1)} %add_rsqrt_fusion), kind=kOutput, calls=%fused_computation.49 | convolution fusion | flops 5240782848 | bytes 15083520 | tf_op jit(solution)/shard_map/dot_general | solution.py:985
  91.1 18.6 %ssm_forward.1 = (f32[1024,768]{1,0:T(8,128)}, f32[1024,768]{1,0:T(8,128)}, bf16[8,128,768]{2,1,0:T(8,128)(2,1)}, f32[8,1024]{1,0:T(8,128)}, f32[1024,1024]{1,0:...) custom-call(f32[1024,1664]{1,0:T(8,128)} %fusion.26.gate_ref.conv_ref.dt_ref.halo_ref, ...), custom_call_target="tpu_custom_call" | custom-call | tf_op jit(solution)/shard_map/ssm_forward/pallas_call | solution.py:162
  109.7 1.4 slice.46.own_ref
  111.0 7.0 %rms_sum.1.rms_ref = f32[1,1024]{1,0:T(1,128)} custom-call(f32[1,1024]{1,0:T(1,128)} %slice.46.own_ref), custom_call_target="tpu_custom_call" | custom-call | tf_op jit(solution)/shard_map/rms_sum/pallas_call | solution.py:673
  118.0 6.9 %fusion.21 = bf16[1024,1536]{1,0:T(8,128)(2,1)} fusion(bf16[1536,768]{1,0:T(8,128)(2,1)} %get-tuple-element.57, f32[1024,768]{1,0:T(8,128)} %get-tuple-element.55, f32[768]{0:T(1024)S(1)} %copy-done.6, f32[1024]{0:T(1024)} %bitcast.62), kind=kOutput, calls=%fused_computation.46 | convolution fusion | flops 2418278400 | bytes 8657920 | tf_op jit(solution)/shard_map/dot_general | solution.py:985
  125.0 0.0 reduce-scatter.3.cloned.1.call-update
  125.0 0.0 reduce-scatter.5.cloned.1.call-start
  125.0 5.7 %pad_maximum_fusion = bf16[1536,1920]{1,0:T(8,128)(2,1)} fusion(bf16[1536,256]{1,0:T(8,128)(2,1)} %bitcast.53, bf16[1536,1664]{1,0:T(8,128)(2,1)} %get-tuple-element.53), kind=kLoop, calls=%fused_computation.8 | loop fusion | flops 11796480 | bytes 11796480 | tf_op jit(solution)/shard_map/concatenate | solution.py:1038
  130.7 5.0 %all-gather.2.cloned.1.call-done = bf16[1024,1536]{1,0:T(8,128)(2,1)} async-done(((bf16[256,1536]{1,0:T(8,128)(2,1)}), bf16[1024,1536]{1,0:T(8,128)(2,1)}) %all-gather.2.cloned.1.call-update) | async-done | bytes 3145744 | tf_op jit(solution)/shard_map/all_gather | solution.py:1007
  135.7 8.0 %multiply_reduce_fusion = (f32[1024]{0:T(1024)S(1)}, f32[1024,768]{1,0:T(8,128)}) fusion(f32[1024,768]{1,0:T(8,128)} %get-tuple-element.55, f32[768]{0:T(1024)S(1)} %copy-done.6, bf16[1024,1536]{1,0:T(8,128)(2,1)} %all-gather.2.cloned.1.call-done, bf16[1536,768]{1,0:T(8,128)(2,1)} %get-tuple-element.57), kind=kOutput, calls=%fused_computation.9 | convolution fusion | flops 2418277376 | bytes 11803648 | tf_op jit(solution)/shard_map/dot_general | solution.py:985
  143.7 0.7 collective-permute-start.2
  144.5 0.3 collective-permute-start.1
  144.8 2.0 collective-permute-start
  146.8 1.0 copy.58.meta_next_ref
  147.8 1.1 collective-permute-done.2
  148.9 0.3 collective-permute-done.1
  149.2 1.2 collective-permute-done
  150.4 0.6 add_add_fusion.dots_ref
  151.0 27.2 %ssm_backward.1 = (bf16[1024,1920]{1,0:T(8,128)(2,1)}, f32[16,1536]{1,0:T(8,128)}) custom-call(f32[1024,1664]{1,0:T(8,128)} %fusion.26.gate_ref.conv_ref.dt_ref.halo_ref, f32[1024,1664]{1,0:T(8,128)} %fusion.26.gate_ref.conv_ref.dt_ref.halo_ref, f32[1024,1664]{1,0:T(8,128)} %fusion.26.gate_ref.conv_ref.dt_ref.halo_ref, ...), custom_call_target="tpu_custom_call" | custom-call | tf_op jit(solution)/shard_map/ssm_backward/pallas_call | solution.py:344
  178.1 11.2 %fusion.4 = (f32[1536]{0:T(1024)S(1)}, bf16[1024,1536]{1,0:T(8,128)(2,1)}) fusion(bf16[1024,1536]{1,0:T(8,128)(2,1)S(1)} %copy-done, f32[1024]{0:T(1024)S(1)} %add_rsqrt_fusion, bf16[1024,1920]{1,0:T(8,128)(2,1)} %get-tuple-element.65, bf16[1536,1920]{1,0:T(8,128)(2,1)} %pad_maximum_fusion), kind=kOutput, calls=%fused_computation.7 | convolution fusion | flops 6047660544 | bytes 16132096 | tf_op jit(solution)/shard_map/dot_general | solution.py:985
  189.4 0.0 reduce-scatter.5.cloned.1.call-update
  189.4 0.9 fusion.19
  190.3 0.7 reshape.146.gain_ref
  191.0 7.3 %fusion.20.go_ref = bf16[1536,768]{1,0:T(8,128)(2,1)} fusion(bf16[1024,1536]{1,0:T(8,128)(2,1)} %all-gather.2.cloned.1.call-done, f32[1024,768]{1,0:T(8,128)} %get-tuple-element.55, f32[768]{0:T(1024)S(1)} %copy-done.6, f32[1024]{0:T(1024)S(1)} %bitcast.63), kind=kOutput, calls=%fused_computation.45 | convolution fusion | flops 2418278400 | bytes 8657920 | tf_op jit(solution)/shard_map/dot_general | solution.py:985
  198.3 0.0 copy-done.12
  198.3 9.0 %fusion.22.ga_ref = bf16[1536,1920]{1,0:T(8,128)(2,1)} fusion(bf16[1024,1920]{1,0:T(8,128)(2,1)S(1)} %copy-done.12, bf16[1024,1536]{1,0:T(8,128)(2,1)S(1)} %copy-done, f32[1536]{0:T(1024)S(1)} %reshape.147, f32[1024]{0:T(1024)S(1)} %add_rsqrt_fusion), kind=kOutput, calls=%fused_computation.47 | convolution fusion | flops 6046089216 | bytes 12986368 | tf_op jit(solution)/shard_map/dot_general | solution.py:985
  207.3 1.4 dynamic_update_slice.3.small_ref
  208.7 51.4 %exit_reduce.1 = (f32[192,1920]{1,0:T(8,128)}, f32[192,768]{1,0:T(8,128)}, f32[48,256]{1,0:T(8,128)}, f32[16,1536]{1,0:T(8,128)}, f32[16,384]{1,0:T(8,128)}) custom-call(bf16[1536,1920]{1,0:T(8,128)(2,1)} %fusion.22.ga_ref, bf16[1536,768]{1,0:T(8,128)(2,1)} %fusion.20.go_ref, f32[16,1536]{1,0:T(8,128)} %dynamic_update_slice.3.small_ref), custom_call_target="tpu_custom_call" | custom-call | tf_op jit(solution)/shard_map/exit_reduce/pallas_call | solution.py:887
  260.2 0.7 slice.50
  260.9 0.6 dynamic_slice.3
  261.5 1.5 reduce-scatter.5.cloned.1.call-done.d_own_ref
  263.0 6.5 %finish.1 = (bf16[256,1536]{1,0:T(8,128)(2,1)}, f32[256,1536]{1,0:T(8,128)}, f32[192,2,768]{2,1,0:T(2,128)}, f32[48,256]{1,0:T(8,128)}, f32[12,192]{1,0:T(8,128)...) custom-call(bf16[256,1536]{1,0:T(8,128)(2,1)} %tok_ref.3, ...), custom_call_target="tpu_custom_call" | custom-call | tf_op jit(solution)/shard_map/finish/pallas_call | solution.py:969
  269.5 0.8 copy.66
  (46 shorter events, 0.2 us)
Async XLA Ops:
  7.2 66.0 %copy-start.3 = (s32[1,1024]{1,0:T(1,128)S(1)}, s32[1,1024]{1,0:T(1,128)}, u32[]{:S(2)}) copy-start(s32[1,1024]{1,0:T(1,128)} %param.17) | copy-start | bytes 12292
  7.2 66.1 %copy-start.6 = (f32[768]{0:T(1024)S(1)}, f32[768]{0:T(1024)}, u32[]{:S(2)}) copy-start(f32[768]{0:T(1024)} %param.30) | copy-start | bytes 9220
  7.2 66.1 %copy-start.13 = (f32[12]{0:T(128)S(1)}, f32[12]{0:T(128)}, u32[]{:S(2)}) copy-start(f32[12]{0:T(128)} %param.28) | copy-start | bytes 148
  7.2 66.2 %copy-start.10 = (f32[12]{0:T(128)S(1)}, f32[12]{0:T(128)}, u32[]{:S(2)}) copy-start(f32[12]{0:T(128)} %param.27) | copy-start | bytes 148
  7.2 66.3 %copy-start.11 = (f32[12]{0:T(128)S(1)}, f32[12]{0:T(128)}, u32[]{:S(2)}) copy-start(f32[12]{0:T(128)} %param.29) | copy-start | bytes 148
  7.2 69.4 %copy-start.9 = (f32[256]{0:T(256)S(1)}, f32[256]{0:T(256)}, u32[]{:S(2)}) copy-start(f32[256]{0:T(256)} %param.26) | copy-start | bytes 3076
  7.2 69.4 %copy-start.7 = (f32[768]{0:T(1024)S(1)}, f32[768]{0:T(1024)}, u32[]{:S(2)}) copy-start(f32[768]{0:T(1024)} %param.24) | copy-start | bytes 9220
  7.3 69.4 %copy-start.8 = (f32[4,256]{1,0:T(4,128)S(1)}, f32[4,256]{1,0:T(4,128)}, u32[]{:S(2)}) copy-start(f32[4,256]{1,0:T(4,128)} %param.25) | copy-start | bytes 12292
  7.3 69.4 %copy-start.5 = (f32[4,768]{1,0:T(4,128)S(1)}, f32[4,768]{1,0:T(4,128)}, u32[]{:S(2)}) copy-start(f32[4,768]{1,0:T(4,128)} %param.23) | copy-start | bytes 36868
  7.3 128.5 %all-gather.2.cloned.1.call-start = ((), (), s32[]{:S(2)}) async-start(), calls=%async_computation.3 | async-start | bytes 3932160 | tf_op jit(solution)/shard_map/all_gather | solution.py:1007
  73.1 7.9 %copy-start = (bf16[1024,1536]{1,0:T(8,128)(2,1)S(1)}, bf16[1024,1536]{1,0:T(8,128)(2,1)}, u32[]{:S(2)}) copy-start(bf16[1024,1536]{1,0:T(8,128)(2,1)} %get-tuple-element.52) | copy-start | bytes 9437188
  73.1 188.4 %reduce-scatter.3.cloned.1.call-start = ((), (), s32[]{:S(2)}) async-start(), calls=%async_computation.2 | async-start | bytes 3932160 | tf_op jit(solution)/shard_map/reduce_scatter | solution.py:1037
  78.0 3.0 %copy-start.1 = (bf16[8,4,48,256]{3,2,1,0:T(8,128)(2,1)S(1)}, bf16[8,4,48,256]{3,2,1,0:T(8,128)(2,1)}, u32[]{:S(2)}) copy-start(bf16[8,4,48,256]{3,2,1,0:T(8,128)(2,1)} %get-tuple-element.54) | copy-start | bytes 2359300
  78.0 5.1 %slice-start = ((s8[5111808]{0:T(1024)(128)(4,1)}), s8[4194304]{0:T(1024)(128)(4,1)S(1)}, s32[]{:S(2)}) async-start(s8[5111808]{0:T(1024)(128)(4,1)} %bitcast.50), calls=%async_computation.5 | async-start | bytes 8388608
  81.0 2.0 slice-start.1
  125.0 138.0 %reduce-scatter.5.cloned.1.call-start = ((), (), s32[]{:S(2)}) async-start(), calls=%async_computation.4 | async-start | bytes 3932160 | tf_op jit(solution)/shard_map/reduce_scatter | solution.py:1054
  143.7 5.2 %collective-permute-start.2 = (f32[1,1024]{1,0:T(1,128)S(1)}, f32[1,1024]{1,0:T(1,128)S(1)}, u32[]{:S(2)}, u32[]{:S(2)}) collective-permute-start(f32[1,1024]{1,0:T(1,128)S(1)} %bitcast.73), channel_id=1, source_target_pairs={{0,3},{1,0},{2,1},{3,2},{4,7},{5,4},{6,5},{7,6},{8,11},{9,8},{10,9... | collective-permute-start | bytes 12296 | tf_op jit(solution)/shard_map/ppermute | solution.py:1044
  144.5 4.7 %collective-permute-start.1 = (f32[1,1024]{1,0:T(1,128)S(1)}, f32[1,1024]{1,0:T(1,128)S(1)}, u32[]{:S(2)}, u32[]{:S(2)}) collective-permute-start(f32[1,1024]{1,0:T(1,128)S(1)} %bitcast.74), channel_id=1, source_target_pairs={{0,2},{1,3},{2,0},{3,1},{4,6},{5,7},{6,4},{7,5},{8,10},{9,11},{10,... | collective-permute-start | bytes 12296 | tf_op jit(solution)/shard_map/ppermute | solution.py:1044
  144.8 5.6 %collective-permute-start = (f32[1,1024]{1,0:T(1,128)S(1)}, f32[1,1024]{1,0:T(1,128)S(1)}, u32[]{:S(2)}, u32[]{:S(2)}) collective-permute-start(f32[1,1024]{1,0:T(1,128)S(1)} %bitcast.75), channel_id=1, source_target_pairs={{0,1},{1,2},{2,3},{3,0},{4,5},{5,6},{6,7},{7,4},{8,9},{9,10},{10,1... | collective-permute-start | bytes 12296 | tf_op jit(solution)/shard_map/ppermute | solution.py:1044
  189.4 1.6 copy-start.4
  191.0 7.3 %copy-start.12 = (bf16[1024,1920]{1,0:T(8,128)(2,1)S(1)}, bf16[1024,1920]{1,0:T(8,128)(2,1)}, u32[]{:S(2)}) copy-start(bf16[1024,1920]{1,0:T(8,128)(2,1)} %get-tuple-element.65) | copy-start | bytes 11796484
  263.0 6.5 %copy-start.2 = (f32[192,768]{1,0:T(8,128)S(1)}, f32[192,768]{1,0:T(8,128)}, u32[]{:S(2)}) copy-start(f32[192,768]{1,0:T(8,128)} %get-tuple-element.86) | copy-start | bytes 1769476
Sparse Core Ops, SparseCore 0:
  73.2 62.4 all-gather.1
  138.0 59.1 reduce-scatter.2
  199.5 63.4 reduce-scatter.4

commit v3 on v2

--- a/solution.py
+++ b/solution.py
@@ -427,8 +427,8 @@
 
 def entry_kernel(
     tensor_size, dp_size,
-    tok_ref, wa_ref, wo_ref, wb_ref, gain_ref, tok_all, wa_all, wo_all, wb_all, gain_all,
-    own_sem, right_send, right_recv, left_send, left_recv,
+    tok_ref, wa_ref, wo_ref, wb_ref, gain_row_ref, tok_all, wa_all, wo_all, wb_all, gain_all,
+    gain_ref, own_sem, right_send, right_recv, left_send, left_recv,
     plane_send, plane_recv, half_send, half_recv, pass_send, pass_recv, small_send, small_recv,
 ):
     line, plane = lax.axis_index("tensor"), lax.axis_index("dp")
@@ -438,6 +438,8 @@
     sibling = {"dp": plane + 1 - 2 * core}
     count = tok_ref.shape[0] // PIECES
     smalls = ((wb_ref, wb_all), (gain_ref, gain_all))
+    gain_ref[...] = jnp.zeros_like(gain_ref)
+    gain_ref[0:1, : gain_row_ref.shape[1]] = gain_row_ref[...].astype(F32)
     greet(tensor_size, dp_size)
 
     def small_out(which, offset):
@@ -629,10 +631,10 @@
             jax.ShapeDtypeStruct((dp_size * wa.shape[0], wa.shape[1]), BF16),
             jax.ShapeDtypeStruct((dp_size * wo.shape[0], wo.shape[1]), BF16),
             jax.ShapeDtypeStruct((dp_size, tensor_size) + wb.shape, BF16),
-            jax.ShapeDtypeStruct((dp_size, tensor_size) + gain.shape, BF16),
+            jax.ShapeDtypeStruct((dp_size, tensor_size, 8, LANES), F32),
         ],
         scratch_shapes=[
-            dma((5,)), *[dma((tensor_size, PIECES))] * 4,
+            pltpu.VMEM((8, LANES), F32), dma((5,)), *[dma((tensor_size, PIECES))] * 4,
             dma((4, chips)), dma((4, chips)), dma((4, 2)), dma((4, 2)), dma((4, chips)), dma((4, chips)),
             dma((2, tensor_size)), dma((2, tensor_size)),
         ],
@@ -913,12 +915,7 @@
 STEPS = 4
 
 
-def finish_kernel(
-    width, bc_rows,
-    tok_ref, cot_ref, gain_ref, mixed_ref, d_own_ref, sa_ref, dt_ref, sb_ref, plane_ref, all_ref,
-    layer_ref, dtok_ref, gzx_ref, gbc_ref, gdt_ref, cxw_ref, cxb_ref, cbw_ref, cbb_ref, dtb_ref, alog_ref, skip_ref,
-    gate_ref,
-):
+def tokens_kernel(tok_ref, cot_ref, gain_ref, mixed_ref, d_own_ref, layer_ref, dtok_ref):
     gain = gain_ref[...]
 
     def step(index, carry):
@@ -926,14 +923,33 @@
         tokens = tok_ref[at, :].astype(F32)
         layer_ref[at, :] = (tokens + mixed_ref[at, :].astype(F32)).astype(BF16)
         inv = lax.rsqrt(jnp.mean(tokens * tokens, -1, keepdims=True) + EPSILON)
-        d_own = d_own_ref[at, :].astype(F32)
-        slope = gain * d_own
+        slope = gain * d_own_ref[at, :].astype(F32)
         dtok_ref[at, :] = cot_ref[at, :].astype(F32) + (
             inv * slope - tokens * (inv * inv * inv) * jnp.mean(tokens * slope, -1, keepdims=True)
         )
         return carry
 
     lax.fori_loop(0, tok_ref.shape[0] // BAND, step, 0)
+
+
+def finish_tokens(tokens, cotangent, gain, mixed, d_own):
+    row = pl.BlockSpec((tokens.shape[0] // STEPS, tokens.shape[1]), lambda i: (i, 0))
+    return pl.pallas_call(
+        tokens_kernel,
+        grid=(STEPS,),
+        in_specs=[row, row, pl.BlockSpec(gain.shape, lambda i: (0, 0)), row, row],
+        out_specs=[row, row],
+        out_shape=[jax.ShapeDtypeStruct(tokens.shape, BF16), jax.ShapeDtypeStruct(tokens.shape, F32)],
+        compiler_params=pltpu.CompilerParams(vmem_limit_bytes=61 * MIB),
+        name="finish_tokens",
+    )(tokens, cotangent, gain, mixed, d_own)
+
+
+def weights_kernel(
+    width, bc_rows,
+    sa_ref, dt_ref, sb_ref, plane_ref, all_ref,
+    gzx_ref, gbc_ref, gdt_ref, cxw_ref, cxb_ref, cbw_ref, cbb_ref, dtb_ref, alog_ref, skip_ref, gate_ref,
+):
     gzx_ref[:, 0, :] = sa_ref[:, :width]
     gzx_ref[:, 1, :] = sa_ref[:, width : 2 * width]
 
@@ -954,26 +970,23 @@
         skip_ref[...] = per_head[0:1, :heads]
 
 
-def finish(width, bc_rows, heads, tokens, cotangent, gain, mixed, d_own, sa, sb, plane_sum, all_sum):
+def finish_weights(width, bc_rows, heads, sa, sb, plane_sum, all_sum):
     row = lambda a: pl.BlockSpec((a[0] // STEPS,) + a[1:], lambda i: (i,) + (0,) * (len(a) - 1))
     last = lambda a: pl.BlockSpec((a[0], LANES), lambda i: (0, 2 * width // LANES))
     fixed = lambda a: pl.BlockSpec(a, lambda i: (0, 0))
     shapes = [
-        (tokens.shape, BF16), (tokens.shape, F32), ((sa.shape[0], 2, width), F32), ((bc_rows, sb.shape[1]), F32),
-        ((heads, sa.shape[0]), F32), ((4, width), F32), ((width // LANES, LANES), F32), ((4, 2 * STATE), F32), ((1, 2 * STATE), F32),
-        ((1, heads), F32), ((1, heads), F32), ((1, heads), F32), ((width // LANES, LANES), F32),
+        (sa.shape[0], 2, width), (bc_rows, sb.shape[1]), (heads, sa.shape[0]), (4, width), (width // LANES, LANES),
+        (4, 2 * STATE), (1, 2 * STATE), (1, heads), (1, heads), (1, heads), (width // LANES, LANES),
     ]
-    kinds = [row, row, row] + [fixed] * 10
-    args = (tokens, cotangent, gain, mixed, d_own, sa, sa, sb, plane_sum, all_sum)
-    inputs = [row, row, fixed, row, row, row, last, fixed, fixed, fixed]
+    args = (sa, sa, sb, plane_sum, all_sum)
     return pl.pallas_call(
-        functools.partial(finish_kernel, width, bc_rows),
+        functools.partial(weights_kernel, width, bc_rows),
         grid=(STEPS,),
-        in_specs=[kind(a.shape) for kind, a in zip(inputs, args)],
-        out_specs=[kind(s[0]) for kind, s in zip(kinds, shapes)],
-        out_shape=[jax.ShapeDtypeStruct(*s) for s in shapes],
+        in_specs=[kind(a.shape) for kind, a in zip([row, last, fixed, fixed, fixed], args)],
+        out_specs=[kind(shape) for kind, shape in zip([row] + [fixed] * 10, shapes)],
+        out_shape=[jax.ShapeDtypeStruct(shape, F32) for shape in shapes],
         compiler_params=pltpu.CompilerParams(vmem_limit_bytes=61 * MIB),
-        name="finish",
+        name="finish_weights",
     )(*args)
 
 
@@ -1001,12 +1014,11 @@
     wa = jnp.concatenate([w_zx.reshape(weight_rows, 2 * width), pad_lanes(w_dt, LANES)], 1)
     wo = w_out.T
     wb = jnp.pad(w_bc, ((0, bc_padded - bc_rows), (0, 0)))
-    gain_block = jnp.broadcast_to(pad_lanes(norm_gain[None], LANES), (16, LANES))
-    tok_all, wa_all, wo_all, wb_all, gain_all = entry(tensor_size, dp_size, tokens, wa, wo, wb, gain_block)
+    tok_all, wa_all, wo_all, wb_all, gain_all = entry(tensor_size, dp_size, tokens, wa, wo, wb, norm_gain[None])
     cot_late, _ = lax.optimization_barrier((cotangent, gain_all))
     d_out = lax.all_gather(cot_late, "tensor", axis=0, tiled=True)
 
-    gain = gain_all[:, :, 0, : norm_gain.shape[0]].reshape(1, model).astype(F32)
+    gain = gain_all[:, :, 0, : norm_gain.shape[0]].reshape(1, model)
     wb_all = wb_all[:, :, :bc_rows].reshape(model, 2 * STATE)
     meta, meta_next, seg_row = token_meta(segment_ids[0])
     channels = width + 2 * STATE
@@ -1044,6 +1056,7 @@
         dots = dots + lax.ppermute(inner_part, "tensor", [(i, (i + step) % tensor_size) for i in range(tensor_size)])
     go = dot(d_out, normed_out, ((0,), (0,)), BF16)
 
+    dots, go = lax.optimization_barrier((dots, go))
     dz, packed = ssm_backward(
         inner, projected, bc_pre, meta, meta_next, seg_row, params, core, d_normed, rms, dots, states, pre, lanes, small_save, model
     )
@@ -1054,9 +1067,10 @@
     d_own = lax.psum_scatter(part, "tensor", scatter_dimension=0, tiled=True)
     ga, part = lax.optimization_barrier((ga, part))
     sa, so, sb, plane_sum, all_sum = leave(tensor_size, dp_size, bc_padded, 2 * STATE, ga, go, packed)
-    layer_out, grad_tokens, gzx, gbc, gdt, cxw, cxb, cbw, cbb, dtb, alog, gsk, ggate = finish(
-        width, bc_rows, heads_here, tokens, cotangent, gain, mixed_own, d_own, sa, sb, plane_sum, all_sum
+    gzx, gbc, gdt, cxw, cxb, cbw, cbb, dtb, alog, gsk, ggate = finish_weights(
+        width, bc_rows, heads_here, sa, sb, plane_sum, all_sum
     )
+    layer_out, grad_tokens = finish_tokens(tokens, cotangent, gain, mixed_own, d_own)
     place = lax.axis_index("dp") * tensor_size + lax.axis_index("tensor")
     own_gain = norm_gain.shape[0]
     return (

time: 278 us -> 275 us (0.989)
  Pallas kernels: 172 us -> 176 us
  waiting for transfers between devices: 9.1 us -> 5.8 us
    pallas_call x1 -> x2, Pallas kernels: 6.51 us -> 9.07 us  [the longest x1 5.07 us: finish_tokens(): pl.pallas_call(tokens_kernel, grid=(STEPS,), in_specs=[row, row, pl.Block...]
  transfers between devices with their start and end apart: 6 -> 6, of which waited for: 5 -> 2; matrix products, arithmetic and copies ran while one was open for 26% -> 26% of each run, Pallas kernels for 38% -> 40%
where the time goes in v3:
time: 275 us; the launch traced here: 274 us
  Pallas kernels  176 us (64%)
  matrix products  51.6 us (19%)
  between operations  14.1 us (5%)
  local copies, waits for them, and re-layouts  12.7 us (5%)
  other arithmetic  11 us (4%)
  waiting for transfers between devices  5.8 us (2%)
  starting transfers between devices  3.17 us (1%)
    pallas_call x1, Pallas kernels, entry(): pl.pallas_call(functools.partial(entry_kernel, tensor_size, dp_size), in_...  61.7 us
    pallas_call x1, Pallas kernels, leave(): pl.pallas_call(functools.partial(exit_kernel, tensor_size, dp_size), in_s...  52.5 us
    dot_general x7, matrix products, dot(): return lax.dot_general(a, b, (dims, ((), ())), preferred_element_type=out)  51.6 us
    pallas_call x1, Pallas kernels, ssm_backward(): pl.pallas_call(functools.partial(backward_kernel, inner), grid=(chunks,),...  27.1 us
    pallas_call x1, Pallas kernels, ssm_forward(): pl.pallas_call(forward_kernel, grid=(chunks,), in_specs=[row(width), row(...  18.6 us
    pallas_call x1, Pallas kernels, stat_sum(): pl.pallas_call(functools.partial(stat_kernel, tensor_size, inner), in_spe...  7.02 us
    concatenate x1, other arithmetic, body(): weights = jnp.concatenate([wa_all, wb_all], 1)  5.68 us
  transfers between devices with their start and end apart: 6, of which 2 were waited for; matrix products, arithmetic and copies ran while one was open for 26% of the time, Pallas kernels for 40%

profile of v3, /device:TPU:0, one launch (start us, length us, event | category | flops | bytes accessed | tf_op | source)
XLA Modules:
  0.0 274.2 jit_solution(15272192773057269215)
XLA Ops:
  7.3 0.0 all-gather.2.cloned.1.call-start
  7.3 0.8 copy.52
  8.2 1.1 copy.63
  9.3 0.9 fusion.6.wa_ref
  10.2 61.7 %entry_gather.1 = (bf16[1024,1536]{1,0:T(8,128)(2,1)}, bf16[1536,1664]{1,0:T(8,128)(2,1)}, bf16[1536,768]{1,0:T(8,128)(2,1)}, bf16[8,4,48,256]{3,2,1,0:T(8,128)(2,1)}, f32[8,4,8,128]{3,2,1,0:T(8,128)}) custom-call(bf16[256,1536]{1,0:T(8,128)(2,1)} %tok_ref.3, bf16[192,1664]{1,0:T(8,128)(2,1)} %fusion.6.wa_ref, bf16[192,768]{1,0:T(8,128)(2,1)} %bitcast.55, ...), custom_call_target="tpu_custom_call" | custom-call | tf_op jit(solution)/shard_map/entry_gather/pallas_call | solution.py:625
  71.8 0.0 all-gather.2.cloned.1.call-update
  71.9 0.0 reduce-scatter.3.cloned.1.call-start
  71.9 0.0 copy-done.3
  71.9 0.1 slice.41
  72.0 0.1 slice.45
  72.1 0.0 copy-done.10
  72.1 0.1 copy.61
  72.2 0.1 copy.62
  72.3 0.1 broadcast_in_dim.30
  72.4 0.1 broadcast_in_dim_reshape.3
  72.5 0.1 add_bitcast_fusion
  72.6 0.6 convert_bitcast_fusion
  73.2 0.1 eq.59
  73.2 0.1 eq.66
  73.3 0.1 fusion.13
  73.4 0.1 stack.58
  73.5 1.0 copy.55.meta_ref
  74.5 1.0 fusion.27
  75.4 0.1 mul.66
  75.5 0.0 copy-done.9
  75.5 0.0 copy-done.7
  75.6 1.3 concatenate.34.params_ref
  76.8 3.0 %fusion = f32[1024]{0:T(1024)S(1)} fusion(bf16[1024,1536]{1,0:T(8,128)(2,1)} %get-tuple-element.54), kind=kLoop, calls=%fused_computation.3 | loop fusion | flops 4717568 | bytes 3149824 | tf_op jit(solution)/shard_map/reduce_sum | solution.py:1039
  79.9 0.0 slice-start.1
  79.9 2.0 fusion.23.bc_ref.bc_halo_ref
  81.9 8.1 %fusion.25.gate_ref.conv_ref.dt_ref.halo_ref = f32[1024,1664]{1,0:T(8,128)} fusion(bf16[1536,1664]{1,0:T(8,128)(2,1)S(1)} %bitcast.49, bf16[1024,1536]{1,0:T(8,128)(2,1)S(1)} %copy-done, f32[1536]{0:T(1024)S(1)} %mul.66, f32[1024]{0:T(1024)S(1)} %add_rsqrt_fusion), kind=kOutput, calls=%fused_computation.47 | convolution fusion | flops 5240782848 | bytes 15083520 | tf_op jit(solution)/shard_map/dot_general | solution.py:998
  90.0 18.6 %ssm_forward.1 = (f32[1024,768]{1,0:T(8,128)}, f32[1024,768]{1,0:T(8,128)}, bf16[8,128,768]{2,1,0:T(8,128)(2,1)}, f32[8,1024]{1,0:T(8,128)}, f32[1024,1024]{1,0:...) custom-call(f32[1024,1664]{1,0:T(8,128)} %fusion.25.gate_ref.conv_ref.dt_ref.halo_ref, ...), custom_call_target="tpu_custom_call" | custom-call | tf_op jit(solution)/shard_map/ssm_forward/pallas_call | solution.py:162
  108.6 1.4 slice.46.own_ref
  110.0 7.0 %rms_sum.1.rms_ref = f32[1,1024]{1,0:T(1,128)} custom-call(f32[1,1024]{1,0:T(1,128)} %slice.46.own_ref), custom_call_target="tpu_custom_call" | custom-call | tf_op jit(solution)/shard_map/rms_sum/pallas_call | solution.py:675
  117.0 6.9 %fusion.20 = bf16[1024,1536]{1,0:T(8,128)(2,1)} fusion(bf16[1536,768]{1,0:T(8,128)(2,1)} %get-tuple-element.59, f32[1024,768]{1,0:T(8,128)} %get-tuple-element.57, f32[768]{0:T(1024)S(1)} %copy-done.6, f32[1024]{0:T(1024)} %bitcast.60), kind=kOutput, calls=%fused_computation.44 | convolution fusion | flops 2418278400 | bytes 8657920 | tf_op jit(solution)/shard_map/dot_general | solution.py:998
  124.0 0.0 reduce-scatter.3.cloned.1.call-update
  124.0 0.0 reduce-scatter.5.cloned.1.call-start
  124.1 1.0 copy.58.meta_next_ref
  125.1 5.7 %pad_maximum_fusion = bf16[1536,1920]{1,0:T(8,128)(2,1)} fusion(bf16[1536,256]{1,0:T(8,128)(2,1)} %bitcast.51, bf16[1536,1664]{1,0:T(8,128)(2,1)} %get-tuple-element.55), kind=kLoop, calls=%fused_computation.8 | loop fusion | flops 11796480 | bytes 11796480 | tf_op jit(solution)/shard_map/concatenate | solution.py:1050
  130.8 3.7 %all-gather.2.cloned.1.call-done = bf16[1024,1536]{1,0:T(8,128)(2,1)} async-done(((bf16[256,1536]{1,0:T(8,128)(2,1)}), bf16[1024,1536]{1,0:T(8,128)(2,1)}) %all-gather.2.cloned.1.call-update) | async-done | bytes 3145744 | tf_op jit(solution)/shard_map/all_gather | solution.py:1019
  134.5 8.1 %multiply_reduce_fusion = (f32[1024]{0:T(1024)S(1)}, f32[1024,768]{1,0:T(8,128)}) fusion(f32[1024,768]{1,0:T(8,128)} %get-tuple-element.57, f32[768]{0:T(1024)S(1)} %copy-done.6, bf16[1024,1536]{1,0:T(8,128)(2,1)} %all-gather.2.cloned.1.call-done, bf16[1536,768]{1,0:T(8,128)(2,1)} %get-tuple-element.59), kind=kOutput, calls=%fused_computation.9 | convolution fusion | flops 2418277376 | bytes 11803648 | tf_op jit(solution)/shard_map/dot_general | solution.py:998
  142.6 0.7 collective-permute-start.2
  143.3 0.3 collective-permute-start.1
  143.6 2.0 collective-permute-start
  145.6 0.0 copy-done.4
  145.6 4.3 %fusion.19.go_ref = bf16[1536,768]{1,0:T(8,128)(2,1)} fusion(bf16[1024,1536]{1,0:T(8,128)(2,1)S(1)} %copy-done.12, f32[1024,768]{1,0:T(8,128)S(1)} %copy-done.13, f32[768]{0:T(1024)S(1)} %copy-done.6, f32[1024]{0:T(1024)S(1)} %bitcast.61), kind=kOutput, calls=%fused_computation.43 | convolution fusion | flops 2418278400 | bytes 8657920 | tf_op jit(solution)/shard_map/dot_general | solution.py:998
  149.9 0.0 collective-permute-done.2
  149.9 0.0 collective-permute-done.1
  149.9 0.0 collective-permute-done
  149.9 0.6 add_add_fusion.dots_ref
  150.5 27.1 %ssm_backward.1 = (bf16[1024,1920]{1,0:T(8,128)(2,1)}, f32[16,1536]{1,0:T(8,128)}) custom-call(f32[1024,1664]{1,0:T(8,128)} %fusion.25.gate_ref.conv_ref.dt_ref.halo_ref, f32[1024,1664]{1,0:T(8,128)} %fusion.25.gate_ref.conv_ref.dt_ref.halo_ref, f32[1024,1664]{1,0:T(8,128)} %fusion.25.gate_ref.conv_ref.dt_ref.halo_ref, ...), custom_call_target="tpu_custom_call" | custom-call | tf_op jit(solution)/shard_map/ssm_backward/pallas_call | solution.py:344
  177.7 11.2 %fusion.4 = (f32[1536]{0:T(1024)S(1)}, bf16[1024,1536]{1,0:T(8,128)(2,1)}) fusion(bf16[1024,1536]{1,0:T(8,128)(2,1)S(1)} %copy-done, f32[1024]{0:T(1024)S(1)} %add_rsqrt_fusion, bf16[1024,1920]{1,0:T(8,128)(2,1)} %get-tuple-element.68, bf16[1536,1920]{1,0:T(8,128)(2,1)} %pad_maximum_fusion), kind=kOutput, calls=%fused_computation.7 | convolution fusion | flops 6047660544 | bytes 16132096 | tf_op jit(solution)/shard_map/dot_general | solution.py:998
  188.9 0.0 reduce-scatter.5.cloned.1.call-update
  188.9 0.7 reshape_squeeze.8.gain_ref
  189.6 10.9 %fusion.21.ga_ref = bf16[1536,1920]{1,0:T(8,128)(2,1)} fusion(bf16[1024,1920]{1,0:T(8,128)(2,1)} %get-tuple-element.68, bf16[1024,1536]{1,0:T(8,128)(2,1)S(1)} %copy-done, f32[1536]{0:T(1024)S(1)} %mul.66, f32[1024]{0:T(1024)S(1)} %add_rsqrt_fusion), kind=kOutput, calls=%fused_computation.45 | convolution fusion | flops 6046089216 | bytes 12986368 | tf_op jit(solution)/shard_map/dot_general | solution.py:998
  200.6 1.4 dynamic_update_slice.3.small_ref
  202.0 52.5 %exit_reduce.1 = (f32[192,1920]{1,0:T(8,128)}, f32[192,768]{1,0:T(8,128)}, f32[48,256]{1,0:T(8,128)}, f32[16,1536]{1,0:T(8,128)}, f32[16,384]{1,0:T(8,128)}) custom-call(bf16[1536,1920]{1,0:T(8,128)(2,1)} %fusion.21.ga_ref, bf16[1536,768]{1,0:T(8,128)(2,1)} %fusion.19.go_ref, f32[16,1536]{1,0:T(8,128)} %dynamic_update_slice.3.small_ref), custom_call_target="tpu_custom_call" | custom-call | tf_op jit(solution)/shard_map/exit_reduce/pallas_call | solution.py:889
  254.5 0.7 slice.50
  255.2 0.6 dynamic_slice.3
  255.8 4.0 %finish_weights.1 = (f32[192,2,768]{2,1,0:T(2,128)}, f32[48,256]{1,0:T(8,128)}, f32[12,192]{1,0:T(8,128)}, f32[4,768]{1,0:T(4,128)}, f32[6,128]{1,0:T(8,128)}, /...) custom-call(f32[192,1920]{1,0:T(8,128)} %get-tuple-element.76.sa_ref, ...), custom_call_target="tpu_custom_call" | custom-call | tf_op jit(solution)/shard_map/finish_weights/pallas_call | solution.py:982
  259.8 0.0 reduce-scatter.3.cloned.1.call-done.mixed_ref
  259.8 2.0 reduce-scatter.5.cloned.1.call-done.d_own_ref
  261.8 5.1 %finish_tokens.1 = (bf16[256,1536]{1,0:T(8,128)(2,1)}, f32[256,1536]{1,0:T(8,128)}) custom-call(bf16[256,1536]{1,0:T(8,128)(2,1)} %tok_ref.3, bf16[256,1536]{1,0:T(8,128)(2,1)} %cot_ref.1, f32[1,1536]{1,0:T(1,128)} %reshape_squeeze.8.gain_ref, bf16[256,1536]{1,0:T(8,128)(2,1)} %reduce-scatter.3.cloned.1.call-done.mixed_ref, ...), custom_call_target="tpu_custom_call" | custom-call | tf_op jit(solution)/shard_map/finish_tokens/pallas_call | solution.py:937
  266.9 0.8 copy.66
  (46 shorter events, 0.2 us)
Async XLA Ops:
  7.2 64.7 %copy-start.3 = (s32[1,1024]{1,0:T(1,128)S(1)}, s32[1,1024]{1,0:T(1,128)}, u32[]{:S(2)}) copy-start(s32[1,1024]{1,0:T(1,128)} %param.17) | copy-start | bytes 12292
  7.2 64.9 %copy-start.6 = (f32[768]{0:T(1024)S(1)}, f32[768]{0:T(1024)}, u32[]{:S(2)}) copy-start(f32[768]{0:T(1024)} %param.30) | copy-start | bytes 9220
  7.2 64.9 %copy-start.14 = (f32[12]{0:T(128)S(1)}, f32[12]{0:T(128)}, u32[]{:S(2)}) copy-start(f32[12]{0:T(128)} %param.28) | copy-start | bytes 148
  7.2 64.9 %copy-start.10 = (f32[12]{0:T(128)S(1)}, f32[12]{0:T(128)}, u32[]{:S(2)}) copy-start(f32[12]{0:T(128)} %param.27) | copy-start | bytes 148
  7.2 65.1 %copy-start.11 = (f32[12]{0:T(128)S(1)}, f32[12]{0:T(128)}, u32[]{:S(2)}) copy-start(f32[12]{0:T(128)} %param.29) | copy-start | bytes 148
  7.2 68.3 %copy-start.9 = (f32[256]{0:T(256)S(1)}, f32[256]{0:T(256)}, u32[]{:S(2)}) copy-start(f32[256]{0:T(256)} %param.26) | copy-start | bytes 3076
  7.2 68.3 %copy-start.7 = (f32[768]{0:T(1024)S(1)}, f32[768]{0:T(1024)}, u32[]{:S(2)}) copy-start(f32[768]{0:T(1024)} %param.24) | copy-start | bytes 9220
  7.3 68.3 %copy-start.8 = (f32[4,256]{1,0:T(4,128)S(1)}, f32[4,256]{1,0:T(4,128)}, u32[]{:S(2)}) copy-start(f32[4,256]{1,0:T(4,128)} %param.25) | copy-start | bytes 12292
  7.3 68.3 %copy-start.5 = (f32[4,768]{1,0:T(4,128)S(1)}, f32[4,768]{1,0:T(4,128)}, u32[]{:S(2)}) copy-start(f32[4,768]{1,0:T(4,128)} %param.23) | copy-start | bytes 36868
  7.3 127.2 %all-gather.2.cloned.1.call-start = ((), (), s32[]{:S(2)}) async-start(), calls=%async_computation.3 | async-start | bytes 3932160 | tf_op jit(solution)/shard_map/all_gather | solution.py:1019
  71.8 8.0 %copy-start = (bf16[1024,1536]{1,0:T(8,128)(2,1)S(1)}, bf16[1024,1536]{1,0:T(8,128)(2,1)}, u32[]{:S(2)}) copy-start(bf16[1024,1536]{1,0:T(8,128)(2,1)} %get-tuple-element.54) | copy-start | bytes 9437188
  71.9 187.9 %reduce-scatter.3.cloned.1.call-start = ((), (), s32[]{:S(2)}) async-start(), calls=%async_computation.2 | async-start | bytes 3932160 | tf_op jit(solution)/shard_map/reduce_scatter | solution.py:1049
  76.8 3.0 %copy-start.1 = (bf16[8,4,48,256]{3,2,1,0:T(8,128)(2,1)S(1)}, bf16[8,4,48,256]{3,2,1,0:T(8,128)(2,1)}, u32[]{:S(2)}) copy-start(bf16[8,4,48,256]{3,2,1,0:T(8,128)(2,1)} %get-tuple-element.56) | copy-start | bytes 2359300
  76.8 5.1 %slice-start = ((s8[5111808]{0:T(1024)(128)(4,1)}), s8[4194304]{0:T(1024)(128)(4,1)S(1)}, s32[]{:S(2)}) async-start(s8[5111808]{0:T(1024)(128)(4,1)} %bitcast.48), calls=%async_computation.5 | async-start | bytes 8388608
  79.9 2.0 slice-start.1
  124.0 137.8 %reduce-scatter.5.cloned.1.call-start = ((), (), s32[]{:S(2)}) async-start(), calls=%async_computation.4 | async-start | bytes 3932160 | tf_op jit(solution)/shard_map/reduce_scatter | solution.py:1067
  130.8 14.8 %copy-start.4 = (f32[1,1024]{1,0:T(1,128)S(1)}, f32[1,1024]{1,0:T(1,128)}, u32[]{:S(2)}) copy-start(f32[1,1024]{1,0:T(1,128)} %rms_sum.1.rms_ref) | copy-start | bytes 12292
  134.5 11.1 %copy-start.12 = (bf16[1024,1536]{1,0:T(8,128)(2,1)S(1)}, bf16[1024,1536]{1,0:T(8,128)(2,1)}, u32[]{:S(2)}) copy-start(bf16[1024,1536]{1,0:T(8,128)(2,1)} %all-gather.2.cloned.1.call-done) | copy-start | bytes 9437188
  134.5 11.1 %copy-start.13 = (f32[1024,768]{1,0:T(8,128)S(1)}, f32[1024,768]{1,0:T(8,128)}, u32[]{:S(2)}) copy-start(f32[1024,768]{1,0:T(8,128)} %get-tuple-element.57) | copy-start | bytes 9437188
  142.6 7.3 %collective-permute-start.2 = (f32[1,1024]{1,0:T(1,128)S(1)}, f32[1,1024]{1,0:T(1,128)S(1)}, u32[]{:S(2)}, u32[]{:S(2)}) collective-permute-start(f32[1,1024]{1,0:T(1,128)S(1)} %bitcast.71), channel_id=1, source_target_pairs={{0,3},{1,0},{2,1},{3,2},{4,7},{5,4},{6,5},{7,6},{8,11},{9,8},{10,9... | collective-permute-start | bytes 12296 | tf_op jit(solution)/shard_map/ppermute | solution.py:1056
  143.3 6.6 %collective-permute-start.1 = (f32[1,1024]{1,0:T(1,128)S(1)}, f32[1,1024]{1,0:T(1,128)S(1)}, u32[]{:S(2)}, u32[]{:S(2)}) collective-permute-start(f32[1,1024]{1,0:T(1,128)S(1)} %bitcast.72), channel_id=1, source_target_pairs={{0,2},{1,3},{2,0},{3,1},{4,6},{5,7},{6,4},{7,5},{8,10},{9,11},{10,... | collective-permute-start | bytes 12296 | tf_op jit(solution)/shard_map/ppermute | solution.py:1056
  143.6 6.3 %collective-permute-start = (f32[1,1024]{1,0:T(1,128)S(1)}, f32[1,1024]{1,0:T(1,128)S(1)}, u32[]{:S(2)}, u32[]{:S(2)}) collective-permute-start(f32[1,1024]{1,0:T(1,128)S(1)} %bitcast.73), channel_id=1, source_target_pairs={{0,1},{1,2},{2,3},{3,0},{4,5},{5,6},{6,7},{7,4},{8,9},{9,10},{10,1... | collective-permute-start | bytes 12296 | tf_op jit(solution)/shard_map/ppermute | solution.py:1056
  255.8 11.1 %copy-start.2 = (f32[192,768]{1,0:T(8,128)S(1)}, f32[192,768]{1,0:T(8,128)}, u32[]{:S(2)}) copy-start(f32[192,768]{1,0:T(8,128)} %get-tuple-element.90) | copy-start | bytes 1769476
Sparse Core Ops, SparseCore 0:
  72.0 62.4 all-gather.1
  136.8 59.1 reduce-scatter.2
  198.3 63.4 reduce-scatter.4
